TPU v7x, 32 devices: a whole 2x2x4 slice. The times are simulated.
32 devices in a mesh: grp: 4 (over y, x), tile: 8 (over z, core).
Axes of the slice: x: 2, y: 2, z: 4, core: 2. Of those that a mesh axis runs over, the one named last changes fastest.
Arguments:
- base_rhs: float32 [1024, 4096], P('grp', 'tile'), may hold values from -6 to 6
- depth: float32 [1024, 4096], P('grp', 'tile'), may hold values from 0.25 to 2
- ssh_prev: float32 [1024, 4096], P('grp', 'tile'), may hold values from -6 to 6
- currents: float32 [2, 1024, 4096], P(None, 'grp', 'tile'), may hold values from -3 to 3
- land_blocks: int32 [128, 512], P('grp', 'tile'), may hold values 0 or 1
- ice_thick: float32 [2, 256, 4096], P(None, 'grp', 'tile'), may hold values from 0.25 to 4
- ice_blocks: int32 [2, 32, 512], P(None, 'grp', 'tile'), may hold values 0 or 1
- ice_vel: float32 [2, 2, 256, 4096], P(None, None, 'grp', 'tile'), may hold values from -3 to 3
- ice_stress: float32 [3, 2, 256, 4096], P(None, None, 'grp', 'tile'), may hold values from -5 to 5
- wind: float32 [2, 2, 256, 4096], P(None, None, 'grp', 'tile'), may hold values from -6 to 6
Outputs:
- ssh: float32 [1024, 4096], P('grp', 'tile')
- ice_vel_out: float32 [2, 2, 256, 4096], P(None, None, 'grp', 'tile')
- ice_stress_out: float32 [3, 2, 256, 4096], P(None, None, 'grp', 'tile')
All inputs are finite; a program needn't handle non-finite values. No bound on the sum of `land_blocks` or of `ice_blocks` on one device may be relied on, other than what follows from the above.
Results may differ from a plain program's by a relative error of at most 0.0001.
Values sent between devices are 32-bit elements; how exact they have to be, the bound alone decides.
A program may use at most 64 MiB of HBM per device.

v0:
```python
import functools

import jax
import jax.numpy as jnp
from jax import lax
from jax.experimental import pallas as pl
from jax.experimental.pallas import tpu as pltpu
from jax.sharding import PartitionSpec as P

BS = 8
NSUB = 8

DAMP = 0.05
RELAX = 0.2
STRENGTH = 0.5
DRAG = 1.0
STEP = 0.5

MESH = pl.DeviceIdType.MESH
F32 = jnp.float32
T = 8
L = 128
W = 12
TOP = 2 * T


def lanes(rows, width):
    return lax.broadcasted_iota(jnp.int32, (rows, width), 1)


def right(x):
    return pltpu.roll(x, x.shape[1] - 1, 1)


def left(x):
    return pltpu.roll(x, 1, 1)


def rows_of(shape):
    return lax.broadcasted_iota(jnp.int32, shape, 0)


def above(prev, here):
    return pltpu.roll(jnp.where(rows_of(here.shape) == T - 1, prev, here), 1, 0)


def below(here, after):
    return pltpu.roll(jnp.where(rows_of(here.shape) == 0, after, here), T - 1, 0)


def kernel(
    groups,
    tiles,
    base_in,
    depth_in,
    ssh_in,
    cur_in,
    land_ref,
    thick_in,
    ice_ref,
    vel_in,
    stress_in,
    wind_in,
    ssh_out,
    vel_out,
    stress_out,
    vel,
    st,
    wind,
    flow,
    h,
    kk,
    pp,
    qq,
    g,
    x,
    b,
    gd,
    v0,
    v1,
    v2,
    w0,
    w1,
    w2,
    wet,
    cover,
    pack_s,
    pack_r,
    opack_s,
    opack_r,
    sp,
    back,
    top_in,
    bot_in,
    red_s,
    red_r,
    red2_s,
    red2_r,
    load_sem,
    flow_send,
    flow_recv,
    row_send,
    row_recv,
    col_send,
    col_recv,
    back_send,
    back_recv,
    edge_send,
    edge_recv,
    red_send,
    red_recv,
    red2_send,
    red2_recv,
    out_sem,
):
    gi = lax.axis_index("grp")
    ti = lax.axis_index("tile")
    rows, cols = thick_in.shape[1], thick_in.shape[2]
    orows = base_in.shape[0]
    wide = cols + L
    end = TOP + rows
    oend = TOP + orows

    loads = []

    def load(src, dst):
        copy = pltpu.make_async_copy(src, dst, load_sem.at[len(loads)])
        copy.start()
        loads.append(copy)
        return copy

    load_thick = load(thick_in, h.at[:, TOP:end, 0:cols])
    load_depth = load(depth_in, g.at[TOP:oend, 0:cols])
    load_x = load(ssh_in, x.at[TOP:oend, 0:cols])
    load_b = load(base_in, b.at[TOP:oend, 0:cols])
    load_vel = load(vel_in, vel.at[:, :, TOP:end, 0:cols])
    load_st = load(stress_in, st.at[:, :, TOP:end, 0:cols])
    load_wind = load(wind_in, wind.at[:, :, TOP:end, 0:cols])

    def clear(ref, top, last, total):
        ref[..., 0:top, :] = jnp.zeros(ref.shape[:-2] + (top, wide), F32)
        ref[..., last:total, :] = jnp.zeros(ref.shape[:-2] + (total - last, wide), F32)
        ref[..., top:last, cols:wide] = jnp.zeros(ref.shape[:-2] + (last - top, L), F32)

    for ref in (vel, st, wind, flow, h):
        clear(ref, TOP, end, end + TOP)
    for ref in (g, x, b):
        clear(ref, TOP, oend, oend + TOP)
    for ref in (pack_r, opack_r):
        ref[...] = jnp.zeros_like(ref)

    barrier = pltpu.get_barrier_semaphore()
    for d in range(1, groups):
        pl.semaphore_signal(
            barrier, inc=1, device_id=(lax.rem(gi + d, groups), ti), device_id_type=MESH
        )
    for d in range(1, tiles):
        pl.semaphore_signal(
            barrier, inc=1, device_id=(gi, lax.rem(ti + d, tiles)), device_id_type=MESH
        )

    def blocks(ref, out, count):
        width = ref.shape[-1]
        row = lax.broadcasted_iota(jnp.int32, (width, cols), 0)
        spread = (row == lax.shift_right_logical(lanes(width, cols), 3)).astype(F32)
        values = ref[...].reshape((count, width)).astype(F32)
        out[...] = jnp.dot(values, spread, preferred_element_type=F32)

    blocks(land_ref, wet, land_ref.shape[0])
    for c in range(2):
        row = lax.broadcasted_iota(jnp.int32, (cols // BS, cols), 0)
        spread = (row == lax.shift_right_logical(lanes(cols // BS, cols), 3)).astype(F32)
        cover[c] = jnp.dot(ice_ref[c].astype(F32), spread, preferred_element_type=F32)

    pl.semaphore_wait(barrier, groups + tiles - 2)

    def flow_copy(cap, target):
        lo = max(0, rows * target - T)
        hi = min(rows * groups, rows * target + rows + T)
        start = TOP + lo - rows * target
        src = cur_in.at[:, lo:hi, :]
        dst = flow.at[:, cap, start : start + hi - lo, 0:cols]
        return src, dst

    homes = (0, groups - 1)
    for cap, home in enumerate(homes):

        @pl.when(gi == home)
        def _():
            order = sorted(range(groups), key=lambda k: -abs(k - home))
            for target in order:
                src, dst = flow_copy(cap, target)
                if target == home:
                    pltpu.make_async_copy(src, dst, flow_recv.at[cap]).start()
                else:
                    pltpu.make_async_remote_copy(
                        src_ref=src,
                        dst_ref=dst,
                        send_sem=flow_send.at[target],
                        recv_sem=flow_recv.at[cap],
                        device_id=(target, ti),
                        device_id_type=MESH,
                    ).start()

    def row_copies(which):
        out = []
        fields = (
            (vel_in, vel, rows, end),
            (stress_in, st, rows, end),
            (wind_in, wind, rows, end),
            (ssh_in, x, orows, oend),
            (base_in, b, orows, oend),
            (h, h, None, end),
            (g, g, None, oend),
        )
        for k, (src, dst, length, last) in enumerate(fields):
            if k not in which:
                continue
            origin = TOP if length is None else 0
            span = (last - TOP) if length is None else length
            lead = (slice(None),) * (len(src.shape) - 2)
            for way in range(2):
                from_row = origin + span - T if way == 0 else origin
                to_row = TOP - T if way == 0 else last
                out.append(
                    (
                        way,
                        pltpu.make_async_remote_copy(
                            src_ref=src.at[lead + (slice(from_row, from_row + T), slice(0, cols))],
                            dst_ref=dst.at[lead + (slice(to_row, to_row + T), slice(0, cols))],
                            send_sem=row_send.at[2 * k + way],
                            recv_sem=row_recv.at[2 * k + way],
                            device_id=(
                                lax.rem(gi + (1 if way == 0 else groups - 1), groups),
                                ti,
                            ),
                            device_id_type=MESH,
                        ),
                    )
                )
        return out

    def edge(way, index, count):
        sends = index < count - 1 if way == 0 else index > 0
        receives = index > 0 if way == 0 else index < count - 1
        return sends, receives

    early = row_copies((0, 1, 2))
    for way, copy in early:
        pl.when(edge(way, gi, groups)[0])(copy.start)

    load_thick.wait()

    def cover_chunk(k, _):
        for c in range(2):
            at = (c, pl.ds(pl.multiple_of(TOP + k * T, T), T), pl.ds(0, cols))
            h[at] = h[at] * cover[c, pl.ds(k, 1), :]
        return 0

    lax.fori_loop(0, rows // T, cover_chunk, 0)
    late = row_copies((5,))
    for way, copy in late:
        pl.when(edge(way, gi, groups)[0])(copy.start)
    load_depth.wait()

    def wet_chunk(k, _):
        at = (pl.ds(pl.multiple_of(TOP + k * T, T), T), pl.ds(0, cols))
        g[at] = g[at] * wet[pl.ds(k, 1), :]
        return 0

    lax.fori_loop(0, orows // T, wet_chunk, 0, unroll=4)
    load_vel.wait()
    load_st.wait()
    load_wind.wait()
    load_x.wait()
    load_b.wait()
    for way, copy in early + late:
        pl.when(edge(way, gi, groups)[1])(copy.wait_recv)

    lane = lanes(T, L)

    def col_copies(src, dst, base):
        out = []
        for way in range(2):
            out.append(
                (
                    way,
                    pltpu.make_async_remote_copy(
                        src_ref=src.at[way],
                        dst_ref=dst.at[way],
                        send_sem=col_send.at[base + way],
                        recv_sem=col_recv.at[base + way],
                        device_id=(gi, lax.rem(ti + (1 if way == 0 else tiles - 1), tiles)),
                        device_id_type=MESH,
                    ),
                )
            )
        return out

    def packed(values):
        after = jnp.zeros((T, L), F32)
        before = jnp.zeros((T, L), F32)
        for f, (first, last) in enumerate(values):
            here = (lane >= W * f) & (lane < W * f + W)
            after = jnp.where(here, pltpu.roll(last, (W * f + W) % L, 1), after)
            before = jnp.where(here, pltpu.roll(first, W * f, 1) if f else first, before)
        return after, before

    def unpacked(from_before, from_after, f):
        low = pltpu.roll(from_before, (L - W - W * f) % L, 1)
        high = pltpu.roll(from_after, (L - W * f) % L, 1) if f else from_after
        return jnp.where(lane < W, high, jnp.where(lane >= L - W, low, 0.0))

    ochunks = orows // T + 2
    ichunks = rows // T + 2

    for target in range(groups):

        @pl.when(gi == target)
        def _():
            for cap, home in enumerate(homes):
                src, dst = flow_copy(cap, target)
                if target == home:
                    pltpu.make_async_copy(src, dst, flow_recv.at[cap]).wait()
                else:
                    pltpu.make_async_remote_copy(
                        src_ref=src,
                        dst_ref=dst,
                        send_sem=flow_send.at[target],
                        recv_sem=flow_recv.at[cap],
                        device_id=(home, ti),
                        device_id_type=MESH,
                    ).wait_recv()

    def ice_fields(c):
        return (
            vel.at[0, c],
            vel.at[1, c],
            st.at[0, c],
            st.at[1, c],
            st.at[2, c],
            h.at[c],
            wind.at[0, c],
            wind.at[1, c],
            flow.at[0, c],
            flow.at[1, c],
        )

    def pack_chunk(k, _):
        at = pl.ds(pl.multiple_of(T + k * T, T), T)
        to = pl.ds(pl.multiple_of(k * T, T), T)
        for c in range(2):
            after, before = packed(
                [(ref[at, pl.ds(0, L)], ref[at, pl.ds(cols - L, L)]) for ref in ice_fields(c)]
            )
            pack_s[0, c, to, :] = after
            pack_s[1, c, to, :] = before
        return 0

    lax.fori_loop(0, ichunks, pack_chunk, 0, unroll=5)
    icols = col_copies(pack_s, pack_r, 2)
    for way, copy in icols:
        pl.when(edge(way, ti, tiles)[0])(copy.start)

    for way, copy in icols:
        pl.when(edge(way, ti, tiles)[1])(copy.wait_recv)

    orow = row_copies((3, 4, 6))
    for way, copy in orow:
        pl.when(edge(way, gi, groups)[0])(copy.start)

    def unpack_chunk(k, _):
        at = pl.ds(pl.multiple_of(T + k * T, T), T)
        to = pl.ds(pl.multiple_of(k * T, T), T)
        for c in range(2):
            for f, ref in enumerate(ice_fields(c)):
                ref[at, pl.ds(cols, L)] = unpacked(pack_r[0, c, to, :], pack_r[1, c, to, :], f)
            thick = h[c, at, :]
            mass = thick + 1.0
            inverse = jnp.where(thick > 0.0, 1.0 / (mass + STEP * DRAG), 0.0)
            q = STEP * inverse
            kk[c, at, :] = (RELAX * STRENGTH / (1.0 + RELAX)) * thick
            pp[c, at, :] = mass * inverse
            qq[c, at, :] = q
            for comp in range(2):
                wind[comp, c, at, :] = q * (wind[comp, c, at, :] + DRAG * flow[comp, c, at, :])
        return 0

    lax.fori_loop(0, ichunks, unpack_chunk, 0, unroll=5)

    keep = 1.0 / (1.0 + RELAX)

    def ice_chunk(k, _):
        r = pl.multiple_of(T + k * T, T)
        at = pl.ds(r, T)
        up = pl.ds(pl.multiple_of(r - T, T), T)
        down = pl.ds(pl.multiple_of(r + T, T), T)
        for c in range(2):
            u = vel[0, c, at, :]
            v = vel[1, c, at, :]
            du_dx = below(u, vel[0, c, down, :]) - u
            dv_dx = below(v, vel[1, c, down, :]) - v
            du_dy = right(u) - u
            dv_dy = right(v) - v
            ed = du_dx + dv_dy
            et = du_dx - dv_dy
            es = du_dy + dv_dx
            inverse = lax.rsqrt(ed * ed + et * et + es * es + 1.0)
            k0 = kk[c, at, :]
            k1 = k0 * inverse
            s0 = st[0, c, at, :] * keep + (k1 * ed - k0)
            s1 = st[1, c, at, :] * keep + k1 * et
            s2 = st[2, c, at, :] * keep + k1 * es
            st[0, c, at, :] = s0
            st[1, c, at, :] = s1
            st[2, c, at, :] = s2
            total = s0 + s1
            diff = s0 - s1
            total_up = above(st[0, c, up, :] + st[1, c, up, :], total)
            s2_up = above(st[2, c, up, :], s2)
            fx = 0.5 * (total - total_up) + (s2 - left(s2))
            fy = 0.5 * (diff - left(diff)) + (s2 - s2_up)
            p = pp[c, at, :]
            q = qq[c, at, :]
            vel[0, c, at, :] = p * u + (q * fx + wind[0, c, at, :])
            vel[1, c, at, :] = p * v + (q * fy + wind[1, c, at, :])
        return 0

    def subcycle(n, _):
        return lax.fori_loop(0, ichunks, ice_chunk, 0, unroll=10)

    lax.fori_loop(0, NSUB // 2, subcycle, 0)

    for way, copy in orow:
        pl.when(edge(way, gi, groups)[1])(copy.wait_recv)

    def opack_chunk(k, _):
        at = pl.ds(pl.multiple_of(T + k * T, T), T)
        to = pl.ds(pl.multiple_of(k * T, T), T)
        after, before = packed(
            [(ref[at, pl.ds(0, L)], ref[at, pl.ds(cols - L, L)]) for ref in (g, x, b)]
        )
        opack_s[0, to, :] = after
        opack_s[1, to, :] = before
        return 0

    lax.fori_loop(0, ochunks, opack_chunk, 0, unroll=17)
    ocols = col_copies(opack_s, opack_r, 0)
    for way, copy in ocols:
        pl.when(edge(way, ti, tiles)[0])(copy.start)

    lax.fori_loop(NSUB // 2, NSUB, subcycle, 0)

    sub = lax.broadcasted_iota(jnp.int32, (T, wide), 0)

    def drag(comp, c, where):
        return jnp.where(
            h[c, where, :] > 0.0, DRAG * (vel[comp, c, where, :] - flow[comp, c, where, :]), 0.0
        )

    def drag_chunk(k, _):
        r = pl.multiple_of(TOP + k * T, T)
        to = pl.ds(pl.multiple_of(k * T, T), T)
        for c in range(2):
            d0 = drag(0, c, pl.ds(r, T))
            d0_up = above(drag(0, c, pl.ds(pl.multiple_of(r - T, T), T)), d0)
            d0_up = jnp.where((sub == 0) & (k == 0), 0.0, d0_up)
            d1 = drag(1, c, pl.ds(r, T))
            sp[c, to, :] = (d0 - d0_up) + (d1 - left(d1))
        return 0

    lax.fori_loop(0, rows // T, drag_chunk, 0, unroll=4)
    for c in range(2):
        sp[c, rows : rows + T, :] = drag(0, c, pl.ds(end - T, T))

    outs = [
        pltpu.make_async_copy(vel.at[:, :, TOP:end, 0:cols], vel_out, out_sem.at[0]),
        pltpu.make_async_copy(st.at[:, :, TOP:end, 0:cols], stress_out, out_sem.at[1]),
    ]

    def back_copy(cap, source, target):
        return pltpu.make_async_remote_copy(
            src_ref=sp.at[cap],
            dst_ref=back.at[source],
            send_sem=back_send.at[cap],
            recv_sem=back_recv.at[source],
            device_id=(target, ti),
            device_id_type=MESH,
        )

    def to_top():
        return pltpu.make_async_remote_copy(
            src_ref=sp.at[0, rows - T : rows + T, :],
            dst_ref=top_in,
            send_sem=edge_send.at[0],
            recv_sem=edge_recv.at[0],
            device_id=(1, ti),
            device_id_type=MESH,
        )

    def to_bot():
        return pltpu.make_async_remote_copy(
            src_ref=sp.at[1, 0:T, :],
            dst_ref=bot_in,
            send_sem=edge_send.at[1],
            recv_sem=edge_recv.at[1],
            device_id=(groups - 2, ti),
            device_id_type=MESH,
        )

    pl.when(gi == groups - 1)(lambda: to_top().start())
    pl.when(gi == 0)(lambda: to_bot().start())
    for cap, home in enumerate(homes):
        for source in range(groups):

            @pl.when(gi == source)
            def _():
                if source == home:
                    pltpu.make_async_copy(
                        sp.at[cap], back.at[source], back_recv.at[source]
                    ).start()
                else:
                    back_copy(cap, source, home).start()

    for copy in outs:
        copy.start()

    for way, copy in ocols:
        pl.when(edge(way, ti, tiles)[1])(copy.wait_recv)

    def ounpack_chunk(k, _):
        at = pl.ds(pl.multiple_of(T + k * T, T), T)
        to = pl.ds(pl.multiple_of(k * T, T), T)
        for f, ref in enumerate((g, x, b)):
            ref[at, pl.ds(cols, L)] = unpacked(opack_r[0, to, :], opack_r[1, to, :], f)
        return 0

    lax.fori_loop(0, ochunks, ounpack_chunk, 0, unroll=17)

    zero = jnp.zeros((T, L), F32)

    def fold(value):
        total = value[:, 0:L]
        for j in range(1, cols // L):
            total = total + value[:, j * L : (j + 1) * L]
        return total

    def owned(k):
        return jnp.where((k >= 1) & (k <= orows // T), 1.0, 0.0).astype(F32)

    def around(ref, r):
        middle = ref[pl.ds(r, T), :]
        up = above(ref[pl.ds(pl.multiple_of(r - T, T), T), :], middle)
        down = below(middle, ref[pl.ds(pl.multiple_of(r + T, T), T), :])
        return (up + down) + (left(middle) + right(middle))

    for ref in (w0, w1, w2):
        ref[0:T, :] = jnp.zeros((T, wide), F32)
        ref[oend + T :, :] = jnp.zeros((T, wide), F32)

    def pre_chunk(k, _):
        r = pl.multiple_of(T + k * T, T)
        at = pl.ds(r, T)
        up, down = pl.ds(pl.multiple_of(r - T, T), T), pl.ds(pl.multiple_of(r + T, T), T)
        g0, gu, gw = g[at, :], g[up, :], g[down, :]
        x_0 = x[at, :]
        gx = g0 * x_0
        g_near = (above(gu, g0) + below(g0, gw)) + (left(g0) + right(g0))
        diag = DAMP + g0 * g_near
        near = (above(gu * x[up, :], gx) + below(gx, gw * x[down, :])) + (left(gx) + right(gx))
        b[at, :] = jnp.where(g0 > 0.0, b[at, :], 0.0) - diag * x_0 + g0 * near
        inverse = 1.0 / diag
        v2[at, :] = inverse
        gd[at, :] = g0 * inverse
        return 0

    lax.fori_loop(0, ochunks, pre_chunk, 0, unroll=2)

    def add(at, value):
        b[at, :] = b[at, :] + jnp.where(g[at, :] > 0.0, value, 0.0)

    for cap, home in enumerate(homes):

        @pl.when(gi == home)
        def _():
            for source in range(groups):
                if source == home:
                    pltpu.make_async_copy(
                        sp.at[cap], back.at[source], back_recv.at[source]
                    ).wait()
                else:
                    back_copy(cap, source, source).wait_recv()
            for source in range(groups):

                def add_chunk(k, _):
                    at = pl.ds(pl.multiple_of(TOP + source * rows + k * T, T), T)
                    add(at, back[source, pl.ds(pl.multiple_of(k * T, T), T), :])
                    return 0

                lax.fori_loop(0, rows // T, add_chunk, 0, unroll=4)
            for source in range(groups):
                row = TOP + (source + 1) * rows
                add(slice(row, row + 1), -back[source, rows + T - 1 : rows + T, :])

    @pl.when(gi == 1)
    def _():
        to_top().wait_recv()
        add(slice(T, TOP), top_in[0:T, :])
        add(slice(TOP, TOP + 1), -top_in[2 * T - 1 : 2 * T, :])

    @pl.when(gi == groups - 2)
    def _():
        to_bot().wait_recv()
        add(slice(oend, oend + T), bot_in[...])

    def first_chunk(k, sums):
        at = pl.ds(pl.multiple_of(T + k * T, T), T)
        r0 = b[at, :]
        z = r0 * v2[at, :]
        v0[at, :] = z
        w0[at, :] = g[at, :] * z
        return sums + owned(k) * fold(r0 * z)

    m0 = lax.fori_loop(0, ochunks, first_chunk, zero, unroll=2)

    def power(w_from, v_to, w_to):
        def chunk(k, sums):
            r = pl.multiple_of(T + k * T, T)
            at = pl.ds(r, T)
            near = around(w_from, r)
            v = gd[at, :] * near
            w = g[at, :] * v
            v_to[at, :] = v
            w_to[at, :] = w
            own = owned(k)
            return (
                sums[0] + own * fold(w_from[at, :] * near),
                sums[1] + own * fold(w * near),
            )

        return lax.fori_loop(0, ochunks, chunk, (zero, zero), unroll=2)

    m1, m2 = power(w0, v1, w1)
    m3, m4 = power(w1, v2, w2)

    def last_chunk(k, sums):
        r = pl.multiple_of(TOP + k * T, T)
        return sums + fold(w2[pl.ds(r, T), :] * around(w2, r))

    m5 = lax.fori_loop(0, orows // T, last_chunk, zero, unroll=2)

    row = lax.broadcasted_iota(jnp.int32, (T, L), 0)
    moments = zero
    for k, m in enumerate((m0, m1, m2, m3, m4, m5)):
        moments = jnp.where(row == k, jnp.sum(m, axis=0, keepdims=True), moments)

    def all_reduce(value, src, dst, send, recv, index, count, device):
        src[...] = value
        for d in range(1, count):
            pltpu.make_async_remote_copy(
                src_ref=src,
                dst_ref=dst.at[d],
                send_sem=send.at[d],
                recv_sem=recv.at[d],
                device_id=device(lax.rem(index + d, count)),
                device_id_type=MESH,
            ).start()
        for d in range(1, count):
            copy = pltpu.make_async_remote_copy(
                src_ref=src,
                dst_ref=dst.at[d],
                send_sem=send.at[d],
                recv_sem=recv.at[d],
                device_id=device(lax.rem(index + d, count)),
                device_id_type=MESH,
            )
            copy.wait()
        for d in range(1, count):
            value = value + dst[d]
        return value

    moments = all_reduce(
        moments, red_s, red_r, red_send, red_recv, ti, tiles, lambda k: (gi, k)
    )
    moments = all_reduce(
        moments, red2_s, red2_r, red2_send, red2_recv, gi, groups, lambda k: (k, ti)
    )
    total = jnp.sum(moments, axis=1, keepdims=True)
    nu = [total[k : k + 1, :] for k in range(6)]
    a = [nu[k] - nu[k + 1] for k in range(5)]

    tiny = 1e-12

    def safe(value, scale):
        ok = value > tiny * scale
        return jnp.where(ok, 1.0 / jnp.where(ok, value, 1.0), 0.0)

    i0 = safe(a[0], 0.0 * a[0])
    l10, l20 = a[1] * i0, a[2] * i0
    d1 = a[2] - l10 * a[1]
    i1 = safe(d1, a[2])
    e21 = a[3] - l20 * a[1]
    l21 = e21 * i1
    d2 = a[4] - l20 * a[2] - l21 * e21
    i2 = safe(d2, a[4])
    y0 = nu[0]
    y1 = nu[1] - l10 * y0
    y2 = nu[2] - l20 * y0 - l21 * y1
    c2 = y2 * i2
    c1 = y1 * i1 - l21 * c2
    c0 = y0 * i0 - l10 * c1 - l20 * c2

    def final_chunk(k, _):
        at = (pl.ds(pl.multiple_of(TOP + k * T, T), T), pl.ds(0, cols))
        x[at] = x[at] + (c0 * v0[at] + (c1 * v1[at] + c2 * v2[at]))
        return 0

    lax.fori_loop(0, orows // T, final_chunk, 0, unroll=4)
    last = pltpu.make_async_copy(x.at[TOP:oend, 0:cols], ssh_out, out_sem.at[2])
    last.start()

    for way, copy in early + late + orow:
        pl.when(edge(way, gi, groups)[0])(copy.wait_send)
    for way, copy in ocols + icols:
        pl.when(edge(way, ti, tiles)[0])(copy.wait_send)
    for cap, home in enumerate(homes):

        @pl.when(gi == home)
        def _():
            for target in range(groups):
                if target != home:
                    src, dst = flow_copy(cap, target)
                    pltpu.make_async_remote_copy(
                        src_ref=src,
                        dst_ref=dst,
                        send_sem=flow_send.at[target],
                        recv_sem=flow_recv.at[cap],
                        device_id=(target, ti),
                        device_id_type=MESH,
                    ).wait_send()

        @pl.when(gi != home)
        def _():
            back_copy(cap, 0, home).wait_send()

    pl.when(gi == groups - 1)(lambda: to_top().wait_send())
    pl.when(gi == 0)(lambda: to_bot().wait_send())
    for copy in outs:
        copy.wait()
    last.wait()


def deliver(*refs):
    half = len(refs) // 2
    for src, dst in zip(refs[:half], refs[half:]):
        dst[...] = src[...]


def step(groups, tiles, *args):
    base_rhs, thick, ice_vel, ice_stress = args[0], args[5], args[7], args[8]
    orows, cols = base_rhs.shape
    rows = thick.shape[1]
    irows = rows + 2 * TOP
    erows = orows + 2 * TOP
    wide = cols + L
    any_spec = pl.BlockSpec(memory_space=pl.ANY)
    hbm = pl.BlockSpec(memory_space=pltpu.HBM)
    vmem = pl.BlockSpec(memory_space=pltpu.VMEM)
    dma = pltpu.SemaphoreType.DMA
    ice = pltpu.VMEM((2, irows, wide), F32)
    ocean = pltpu.VMEM((erows, wide), F32)
    results = pl.pallas_call(
        functools.partial(kernel, groups, tiles),
        out_shape=(
            jax.ShapeDtypeStruct(base_rhs.shape, F32),
            jax.ShapeDtypeStruct(ice_vel.shape, F32),
            jax.ShapeDtypeStruct(ice_stress.shape, F32),
        ),
        in_specs=[hbm] * 4 + [vmem, hbm, vmem] + [hbm] * 3,
        out_specs=(any_spec,) * 3,
        scratch_shapes=[
            pltpu.VMEM((2, 2, irows, wide), F32),
            pltpu.VMEM((3, 2, irows, wide), F32),
            pltpu.VMEM((2, 2, irows, wide), F32),
            pltpu.VMEM((2, 2, irows, wide), F32),
            ice,
            ice,
            ice,
            ice,
        ]
        + [ocean] * 10
        + [
            pltpu.VMEM((orows // BS, cols), F32),
            pltpu.VMEM((2, rows // BS, cols), F32),
            pltpu.VMEM((2, 2, rows + 2 * T, L), F32),
            pltpu.VMEM((2, 2, rows + 2 * T, L), F32),
            pltpu.VMEM((2, orows + 2 * T, L), F32),
            pltpu.VMEM((2, orows + 2 * T, L), F32),
            pltpu.VMEM((2, rows + T, wide), F32),
            pltpu.VMEM((groups, rows + T, wide), F32),
            pltpu.VMEM((2 * T, wide), F32),
            pltpu.VMEM((T, wide), F32),
            pltpu.VMEM((T, L), F32),
            pltpu.VMEM((tiles, T, L), F32),
            pltpu.VMEM((T, L), F32),
            pltpu.VMEM((groups, T, L), F32),
            dma((7,)),
            dma((groups,)),
            dma((2,)),
            dma((14,)),
            dma((14,)),
            dma((4,)),
            dma((4,)),
            dma((2,)),
            dma((groups,)),
            dma((2,)),
            dma((2,)),
            dma((tiles,)),
            dma((tiles,)),
            dma((groups,)),
            dma((groups,)),
            dma((3,)),
        ],
        compiler_params=pltpu.CompilerParams(
            collective_id=0, has_side_effects=True, vmem_limit_bytes=67_043_328
        ),
    )(*args)
    return pl.pallas_call(
        deliver,
        out_shape=tuple(jax.ShapeDtypeStruct(r.shape, F32) for r in results),
        in_specs=[vmem] * 3,
        out_specs=(vmem,) * 3,
    )(*results)


def solution(mesh):
    grid = P("grp", "tile")
    plane = P(None, "grp", "tile")
    stack = P(None, None, "grp", "tile")
    return jax.shard_map(
        functools.partial(step, mesh.shape["grp"], mesh.shape["tile"]),
        mesh=mesh,
        in_specs=(grid, grid, grid, plane, grid, plane, plane, stack, stack, stack),
        out_specs=(grid, stack, stack),
        check_vma=False,
    )
```

profile of v0, /device:TPU:0, one launch (start us, length us, event | category | flops | bytes accessed | tf_op | source)
XLA Modules:
  0.0 69.0 jit_solution(18355170356246606947)
XLA Ops:
  0.6 65.6 %shard_map.121 = (f32[256,512]{1,0:T(8,128)}, f32[2,2,64,512]{3,2,1,0:T(8,128)}, f32[3,2,64,512]{3,2,1,0:T(8,128)}) custom-call(f32[256,512]{1,0:T(8,128)} %base_in.1, f32[256,512]{1,0:T(8,128)} %depth_in.1, f32[256,512]{1,0:T(8,128)} %ssh_in.1, f32[2,256,512]{2,1,0:T(8,128)} %cur_in.1, s32[32,64]{1,0:T(8,128)} %land_ref.1, f32[2,64,512]{2,1,0:T(8,128)} %thick_in.1, ...), custom_call_target="tpu_custom_call" | custom-call | tf_op jit(solution)/shard_map/pallas_call | solution.py:772
  66.3 2.7 %shard_map.122 = (f32[256,512]{1,0:T(8,128)}, f32[2,2,64,512]{3,2,1,0:T(8,128)}, f32[3,2,64,512]{3,2,1,0:T(8,128)}) custom-call(f32[256,512]{1,0:T(8,128)} %get-tuple-element.6.refs_0_, f32[2,2,64,512]{3,2,1,0:T(8,128)} %get-tuple-element.7.refs_1_, f32[3,2,64,512]{3,2,1,0:T(8,128)} %get-tuple-element.8.refs_2_), custom_call_target="tpu_custom_call" | custom-call | tf_op jit(solution)/shard_map/pallas_call | solution.py:828
where the time goes:
time: 69.3 us; the launch traced here: 69 us
  Pallas kernels  68.3 us (99%)
    pallas_call x1, Pallas kernels, step(): pl.pallas_call(functools.partial(kernel, groups, tiles), out_shape=(jax.S...  65.6 us
    pallas_call x1, Pallas kernels, step(): pl.pallas_call(deliver, out_shape=tuple((jax.ShapeDtypeStruct(r.shape, F3...  2.71 us

commit v1 on v0

v1 whole, which is shorter than its diff:
```python
import functools
import math

import jax
import jax.numpy as jnp
from jax import lax
from jax.experimental import pallas as pl
from jax.experimental.pallas import tpu as pltpu
from jax.sharding import PartitionSpec as P

BS = 8
NSUB = 8

DAMP = 0.05
RELAX = 0.2
STRENGTH = 0.5
DRAG = 1.0
STEP = 0.5
KEEP = 1.0 / (1.0 + RELAX)
RATE = math.sqrt(2.0) * RELAX * STRENGTH / (1.0 + RELAX)

MESH = pl.DeviceIdType.MESH
F32 = jnp.float32
T = 8
L = 128
W = 12
TOP = 2 * T
PAD = 2 * T


def lanes(rows, width):
    return lax.broadcasted_iota(jnp.int32, (rows, width), 1)


def above(prev, here):
    row = lax.broadcasted_iota(jnp.int32, here.shape, 0)
    return pltpu.roll(jnp.where(row == T - 1, prev, here), 1, 0)


def turn_right(tiles):
    return [pltpu.roll(x, L - 1, 1) for x in tiles]


def turn_left(tiles):
    return [pltpu.roll(x, 1, 1) for x in tiles]


def join_right(turned):
    lane = lanes(T, L)
    n = len(turned)
    return [jnp.where(lane == L - 1, turned[(j + 1) % n], turned[j]) for j in range(n)]


def join_left(turned):
    lane = lanes(T, L)
    n = len(turned)
    return [jnp.where(lane == 0, turned[(j - 1) % n], turned[j]) for j in range(n)]


def right(tiles):
    return join_right(turn_right(tiles))


def left(tiles):
    return join_left(turn_left(tiles))


def kernel(
    groups,
    tiles,
    base_in,
    depth_in,
    ssh_in,
    cur_in,
    land_ref,
    thick_in,
    ice_ref,
    vel_in,
    stress_in,
    wind_in,
    ssh_out,
    vel_out,
    stress_out,
    vel,
    st,
    wind,
    flow,
    h,
    gn,
    xn,
    bn,
    uu,
    vv,
    sp_p,
    sp_m,
    sp_s,
    kk,
    pp,
    qq,
    ww,
    flow_edge,
    g,
    gx,
    r0,
    x,
    inv,
    gd,
    forcing,
    v0,
    v1,
    v2,
    w0,
    w1,
    w2,
    wet,
    cover,
    pack_s,
    pack_r,
    fpack_s,
    fpack_r,
    opack_s,
    opack_r,
    sp,
    extra,
    red_s,
    red_r,
    red2_s,
    red2_r,
    load_sem,
    flow_send,
    flow_recv,
    row_send,
    row_recv,
    col_send,
    col_recv,
    back_send,
    back_recv,
    edge_send,
    edge_recv,
    red_send,
    red_recv,
    red2_send,
    red2_recv,
    out_sem,
):
    gi = lax.axis_index("grp")
    ti = lax.axis_index("tile")
    rows, cols = thick_in.shape[1], thick_in.shape[2]
    orows = base_in.shape[0]
    end = TOP + rows
    oend = TOP + orows
    own = cols // L
    span = own + 1
    ichunks = rows // T + 2
    ochunks = orows // T + 2

    loads = []

    def load(src, dst):
        copy = pltpu.make_async_copy(src, dst, load_sem.at[len(loads)])
        copy.start()
        loads.append(copy)
        return copy

    load_thick = load(thick_in, h.at[:, TOP:end, :])
    load_depth = load(depth_in, gn.at[TOP:oend, :])
    load_x = load(ssh_in, xn.at[TOP:oend, :])
    load_b = load(base_in, bn.at[TOP:oend, :])
    load_vel = load(vel_in, vel.at[:, :, TOP:end, :])
    load_st = load(stress_in, st.at[:, :, TOP:end, :])
    load_wind = load(wind_in, wind.at[:, :, TOP:end, :])

    def clear(ref, *spans):
        for lo, hi in spans:
            ref[..., lo:hi, :] = jnp.zeros(ref.shape[:-2] + (hi - lo, ref.shape[-1]), F32)

    for ref in (vel, st, wind, flow, h):
        clear(ref, (T, TOP), (end, end + T))
    for ref in (gn, xn, bn):
        clear(ref, (T, TOP), (oend, oend + T))
    for ref in (pack_r, fpack_r, opack_r, forcing):
        ref[...] = jnp.zeros_like(ref)

    barrier = pltpu.get_barrier_semaphore()
    for d in range(1, groups):
        pl.semaphore_signal(
            barrier, inc=1, device_id=(lax.rem(gi + d, groups), ti), device_id_type=MESH
        )
    for d in range(1, tiles):
        pl.semaphore_signal(
            barrier, inc=1, device_id=(gi, lax.rem(ti + d, tiles)), device_id_type=MESH
        )

    for ref in (uu, vv, sp_p, sp_m, sp_s):
        clear(ref, (0, T), (end + T, end + 2 * T))
    for ref in (g, gx, w0, w1, w2):
        clear(ref, (0, T), (oend + T, oend + 2 * T))

    def blocks(ref, out, count):
        width = ref.shape[-1]
        row = lax.broadcasted_iota(jnp.int32, (width, cols), 0)
        spread = (row == lax.shift_right_logical(lanes(width, cols), 3)).astype(F32)
        values = ref[...].reshape((count, width)).astype(F32)
        out[...] = jnp.dot(values, spread, preferred_element_type=F32)

    blocks(land_ref, wet, land_ref.shape[0])
    for c in range(2):
        row = lax.broadcasted_iota(jnp.int32, (cols // BS, cols), 0)
        spread = (row == lax.shift_right_logical(lanes(cols // BS, cols), 3)).astype(F32)
        cover[c] = jnp.dot(ice_ref[c].astype(F32), spread, preferred_element_type=F32)

    pl.semaphore_wait(barrier, groups + tiles - 2)

    homes = (0, groups - 1)
    pieces = ((0, L), (cols - L, cols), (L, cols - L))

    def flow_copy(cap, target, piece):
        lo = max(0, rows * target - T)
        hi = min(rows * groups, rows * target + rows + T)
        start = TOP + lo - rows * target
        first, last = pieces[piece]
        src = cur_in.at[:, lo:hi, first:last]
        dst = flow.at[:, cap, start : start + hi - lo, first:last]
        if target == homes[cap]:
            return pltpu.make_async_copy(src, dst, flow_recv.at[3 * cap + piece])
        return pltpu.make_async_remote_copy(
            src_ref=src,
            dst_ref=dst,
            send_sem=flow_send.at[3 * target + piece],
            recv_sem=flow_recv.at[3 * cap + piece],
            device_id=(target, ti),
            device_id_type=MESH,
        )

    def row_copies(which):
        out = []
        fields = (
            (vel_in, vel, rows, end),
            (stress_in, st, rows, end),
            (wind_in, wind, rows, end),
            (ssh_in, xn, orows, oend),
            (base_in, bn, orows, oend),
            (h, h, None, end),
            (gn, gn, None, oend),
        )
        for k, (src, dst, length, last) in enumerate(fields):
            if k not in which:
                continue
            origin = TOP if length is None else 0
            count = (last - TOP) if length is None else length
            lead = (slice(None),) * (len(src.shape) - 2)
            for way in range(2):
                from_row = origin + count - T if way == 0 else origin
                to_row = TOP - T if way == 0 else last
                out.append(
                    (
                        way,
                        pltpu.make_async_remote_copy(
                            src_ref=src.at[lead + (slice(from_row, from_row + T), slice(0, cols))],
                            dst_ref=dst.at[lead + (slice(to_row, to_row + T), slice(0, cols))],
                            send_sem=row_send.at[2 * k + way],
                            recv_sem=row_recv.at[2 * k + way],
                            device_id=(
                                lax.rem(gi + (1 if way == 0 else groups - 1), groups),
                                ti,
                            ),
                            device_id_type=MESH,
                        ),
                    )
                )
        return out

    def edge(way, index, count):
        sends = index < count - 1 if way == 0 else index > 0
        receives = index > 0 if way == 0 else index < count - 1
        return sends, receives

    def start_all(copies, index, count):
        for way, copy in copies:
            pl.when(edge(way, index, count)[0])(copy.start)

    def receive_all(copies, index, count):
        for way, copy in copies:
            pl.when(edge(way, index, count)[1])(copy.wait_recv)

    early = row_copies((0, 1, 2))
    start_all(early, gi, groups)

    for cap, home in enumerate(homes):

        @pl.when(gi == home)
        def _():
            for piece in range(3):
                flow_copy(cap, home, piece).start()

    load_thick.wait()

    def cover_chunk(k, _):
        for c in range(2):
            at = (c, pl.ds(pl.multiple_of(TOP + k * T, T), T), slice(None))
            h[at] = h[at] * cover[c, pl.ds(k, 1), :]
        return 0

    lax.fori_loop(0, rows // T, cover_chunk, 0, unroll=4)
    late = row_copies((5,))
    start_all(late, gi, groups)

    load_depth.wait()

    def wet_chunk(k, _):
        at = (pl.ds(pl.multiple_of(TOP + k * T, T), T), slice(None))
        gn[at] = gn[at] * wet[pl.ds(k, 1), :]
        return 0

    lax.fori_loop(0, orows // T, wet_chunk, 0, unroll=4)
    orow = row_copies((3, 4, 6))
    start_all(orow, gi, groups)

    for cap, home in enumerate(homes):

        @pl.when(gi == home)
        def _():
            order = sorted((k for k in range(groups) if k != home), key=lambda k: abs(k - home))
            for target in order[1:] + order[:1]:
                for piece in range(3):
                    flow_copy(cap, target, piece).start()

    load_vel.wait()
    load_st.wait()
    load_wind.wait()
    load_x.wait()
    load_b.wait()
    receive_all(early + late, gi, groups)

    lane = lanes(T, L)

    def col_copies(src, dst, base):
        out = []
        for way in range(2):
            out.append(
                (
                    way,
                    pltpu.make_async_remote_copy(
                        src_ref=src(way),
                        dst_ref=dst(way),
                        send_sem=col_send.at[base + way],
                        recv_sem=col_recv.at[base + way],
                        device_id=(gi, lax.rem(ti + (1 if way == 0 else tiles - 1), tiles)),
                        device_id_type=MESH,
                    ),
                )
            )
        return out

    def packed(values):
        after = jnp.zeros((T, L), F32)
        before = jnp.zeros((T, L), F32)
        for f, (first, last) in enumerate(values):
            here = (lane >= W * f) & (lane < W * f + W)
            after = jnp.where(here, pltpu.roll(last, (W * f + W) % L, 1), after)
            before = jnp.where(here, pltpu.roll(first, W * f, 1) if f else first, before)
        return after, before

    def unpacked(from_before, from_after, f):
        low = pltpu.roll(from_before, (L - W - W * f) % L, 1)
        high = pltpu.roll(from_after, (L - W * f) % L, 1) if f else from_after
        return jnp.where(lane < W, high, jnp.where(lane >= L - W, low, 0.0))

    def ends(refs, at):
        return [(ref[at, pl.ds(0, L)], ref[at, pl.ds(cols - L, L)]) for ref in refs]

    def ice_fields(c):
        return (
            vel.at[0, c],
            vel.at[1, c],
            st.at[0, c],
            st.at[1, c],
            st.at[2, c],
            h.at[c],
            wind.at[0, c],
            wind.at[1, c],
        )

    def chunk(k):
        return pl.ds(pl.multiple_of(T + k * T, T), T)

    def chunk0(k):
        return pl.ds(pl.multiple_of(k * T, T), T)

    def pack_chunk(k, _):
        for c in range(2):
            after, before = packed(ends(ice_fields(c), chunk(k)))
            pack_s[0, c, chunk0(k), :] = after
            pack_s[1, c, chunk0(k), :] = before
        return 0

    lax.fori_loop(0, ichunks, pack_chunk, 0, unroll=5)
    icols = col_copies(lambda way: pack_s.at[way], lambda way: pack_r.at[way], 0)
    start_all(icols, ti, tiles)

    receive_all(orow, gi, groups)

    def opack_chunk(k, _):
        after, before = packed(ends((gn, xn, bn), chunk(k)))
        opack_s[0, chunk0(k), :] = after
        opack_s[1, chunk0(k), :] = before
        return 0

    lax.fori_loop(0, ochunks, opack_chunk, 0, unroll=17 if ochunks % 17 == 0 else 1)
    ocols = col_copies(lambda way: opack_s.at[way], lambda way: opack_r.at[way], 2)
    start_all(ocols, ti, tiles)

    receive_all(icols, ti, tiles)

    def prep(c):
        def body(k, thick_up):
            at = chunk(k)
            fields = ice_fields(c)
            values = [[ref[at, pl.ds(j * L, L)] for ref in fields] for j in range(own)]
            before, after = pack_r[0, c, chunk0(k), :], pack_r[1, c, chunk0(k), :]
            values.append([unpacked(before, after, f) for f in range(len(fields))])
            thicks = [v[5] for v in values]
            beside = left(thicks)
            for j, (u, v, s0, s1, s2, thick, wx, wy) in enumerate(values):
                mass = thick + 1.0
                inverse = jnp.where(thick > 0.0, 1.0 / (mass + STEP * DRAG), 0.0)
                q = STEP * inverse
                half = 0.5 * q
                uu[c, j, at, :] = u
                vv[c, j, at, :] = v
                sp_p[c, j, at, :] = (s0 + s1) + STRENGTH * thick
                sp_m[c, j, at, :] = (s0 - s1) + STRENGTH * thick
                sp_s[c, j, at, :] = s2 + s2
                kk[c, j, at, :] = RATE * thick
                pp[c, j, at, :] = mass * inverse
                qq[c, j, at, :] = half
                slope = STRENGTH * half
                ww[0, c, j, at, :] = q * wx - slope * (thick - above(thick_up[j], thick))
                ww[1, c, j, at, :] = q * wy - slope * (thick - beside[j])
            return tuple(thicks)

        zero = jnp.zeros((T, L), F32)
        lax.fori_loop(0, ichunks, body, (zero,) * span, unroll=2)

    prep(0)
    prep(1)

    receive_all(ocols, ti, tiles)

    def ocean_chunk(k, _):
        at = chunk(k)
        before, after = opack_r[0, chunk0(k), :], opack_r[1, chunk0(k), :]
        values = [[ref[at, pl.ds(j * L, L)] for ref in (gn, xn, bn)] for j in range(own)]
        values.append([unpacked(before, after, f) for f in range(3)])
        for j, (depth, height, base) in enumerate(values):
            g[j, at, :] = depth
            gx[j, at, :] = depth * height
            x[j, at, :] = height
            r0[j, at, :] = jnp.where(depth > 0.0, base, 0.0)
        return 0

    lax.fori_loop(0, ochunks, ocean_chunk, 0, unroll=2)

    def around(ref, k, lefts, rights):
        r = T + k * T
        up, down = pl.ds(r - 1, T), pl.ds(r + 1, T)
        lefts, rights = join_left(lefts), join_right(rights)
        return [
            (ref[j, up, :] + ref[j, down, :]) + (lefts[j] + rights[j]) for j in range(span)
        ]

    def turned(ref, k):
        values = [ref[j, chunk(k), :] for j in range(span)]
        return turn_left(values), turn_right(values)

    def pre_chunk(k, _):
        at = chunk(k)
        g_near = around(g, k, *turned(g, k))
        near = around(gx, k, *turned(gx, k))
        for j in range(span):
            depth = g[j, at, :]
            diag = DAMP + depth * g_near[j]
            inverse = 1.0 / diag
            r0[j, at, :] = r0[j, at, :] - diag * x[j, at, :] + depth * near[j]
            inv[j, at, :] = inverse
            gd[j, at, :] = depth * inverse
        return 0

    lax.fori_loop(0, ochunks, pre_chunk, 0, unroll=2)

    def ice_cap(phase):
        c = lax.rem(gi + phase, 2)


        def flow_wait(which):
            for target in range(groups):

                @pl.when(gi == target)
                def _():
                    cap = (target + phase) % 2
                    for piece in which:
                        copy = flow_copy(cap, target, piece)
                        if target == homes[cap]:
                            copy.wait()
                        else:
                            copy.wait_recv()

        flow_wait((0, 1))

        def fpack_chunk(k, _):
            after, before = packed(ends((flow.at[0, c], flow.at[1, c]), chunk(k)))
            fpack_s[0, c, chunk0(k), :] = after
            fpack_s[1, c, chunk0(k), :] = before
            return 0

        lax.fori_loop(0, ichunks, fpack_chunk, 0, unroll=ichunks)
        fcols = col_copies(
            lambda way: fpack_s.at[way, c], lambda way: fpack_r.at[way, c], 4 + 2 * phase
        )
        start_all(fcols, ti, tiles)
        flow_wait((2,))
        receive_all(fcols, ti, tiles)

        def flow_chunk(k, _):
            at = chunk(k)
            before, after = fpack_r[0, c, chunk0(k), :], fpack_r[1, c, chunk0(k), :]
            for comp in range(2):
                values = [flow[comp, c, at, pl.ds(j * L, L)] for j in range(own)]
                values.append(unpacked(before, after, comp))
                flow_edge[comp, c, at, :] = values[own]
                for j in range(span):
                    ww[comp, c, j, at, :] = ww[comp, c, j, at, :] + qq[c, j, at, :] * (
                        2.0 * DRAG * values[j]
                    )
            return 0

        lax.fori_loop(0, ichunks, flow_chunk, 0, unroll=ichunks)

        def subcycle(n, _):
            ahead, behind = 2, 2
            turned_u, turned_v, turned_m, turned_s = {}, {}, {}, {}

            def look(k):
                at = slice(T + T * k, TOP + T * k)
                turned_u[k] = turn_right([uu[c, j, at, :] for j in range(span)])
                turned_v[k] = turn_right([vv[c, j, at, :] for j in range(span)])

            def stress(k):
                at, down = slice(T + T * k, TOP + T * k), slice(T + T * k + 1, TOP + T * k + 1)
                beside_u, beside_v = join_right(turned_u.pop(k)), join_right(turned_v.pop(k))
                ms, ss = [], []
                for j in range(span):
                    u, v = uu[c, j, at, :], vv[c, j, at, :]
                    du = uu[c, j, down, :] - u
                    dv = beside_v[j] - v
                    shear = (beside_u[j] - u) + (vv[c, j, down, :] - v)
                    rate = kk[c, j, at, :] * lax.rsqrt(
                        (du * du + dv * dv) + (0.5 * (shear * shear) + 0.5)
                    )
                    sp_p[c, j, at, :] = sp_p[c, j, at, :] * KEEP + rate * du
                    m = sp_m[c, j, at, :] * KEEP + rate * dv
                    s = sp_s[c, j, at, :] * KEEP + rate * shear
                    sp_m[c, j, at, :] = m
                    sp_s[c, j, at, :] = s
                    ms.append(m)
                    ss.append(s)
                turned_m[k], turned_s[k] = turn_left(ms), turn_left(ss)

            def momentum(k):
                at, up = slice(T + T * k, TOP + T * k), slice(T + T * k - 1, TOP + T * k - 1)
                beside_m, beside_s = join_left(turned_m.pop(k)), join_left(turned_s.pop(k))
                for j in range(span):
                    s = sp_s[c, j, at, :]
                    fx = (sp_p[c, j, at, :] - sp_p[c, j, up, :]) + (s - beside_s[j])
                    fy = (sp_m[c, j, at, :] - beside_m[j]) + (s - sp_s[c, j, up, :])
                    p, q = pp[c, j, at, :], qq[c, j, at, :]
                    uu[c, j, at, :] = p * uu[c, j, at, :] + (q * fx + ww[0, c, j, at, :])
                    vv[c, j, at, :] = p * vv[c, j, at, :] + (q * fy + ww[1, c, j, at, :])

            for k in range(-ahead, ichunks + behind):
                if k + ahead < ichunks:
                    look(k + ahead)
                if 0 <= k < ichunks:
                    stress(k)
                if 0 <= k - behind < ichunks:
                    momentum(k - behind)
            return 0

        lax.fori_loop(0, NSUB, subcycle, 0)

        def drag_chunk(k, drag_up):
            at = pl.ds(pl.multiple_of(TOP + k * T, T), T)
            drags = []
            for comp, ref in enumerate((uu, vv)):
                values = [flow[comp, c, at, pl.ds(j * L, L)] for j in range(own)]
                values.append(flow_edge[comp, c, at, :])
                drags.append(
                    [
                        jnp.where(qq[c, j, at, :] > 0.0, DRAG * (ref[c, j, at, :] - values[j]), 0.0)
                        for j in range(span)
                    ]
                )
            beside = left(drags[1])
            for j in range(span):
                d0 = drags[0][j]
                d0_up = above(jnp.zeros((T, L), F32) if drag_up is None else drag_up[j], d0)
                sp[c, j, chunk0(k), :] = (d0 - d0_up) + (drags[1][j] - beside[j])
            return tuple(drags[0])

        zero = jnp.zeros((T, L), F32)
        last = lax.fori_loop(0, rows // T, drag_chunk, (zero,) * span, unroll=rows // T)
        for j in range(span):
            sp[c, j, rows : rows + T, :] = last[j]

        home = c * (groups - 1)

        @pl.when(gi != home)
        def _():
            for copy in back_copies(phase, c, gi, home):
                copy.start()

        @pl.when(gi == home)
        def _():
            row = pl.multiple_of(TOP + gi * rows, T)
            for j in range(span):

                def own_chunk(k, _):
                    forcing[j, pl.ds(pl.multiple_of(row + k * T, T), T), :] = sp[c, j, chunk0(k), :]
                    return 0

                lax.fori_loop(0, rows // T, own_chunk, 0, unroll=rows // T)
                extra[gi, j] = sp[c, j, rows : rows + T, :]

        if phase == 1:
            for copy in edge_copies():
                pl.when(gi == copy[0])(copy[2].start)

        def out_chunk(k, _):
            at = pl.ds(pl.multiple_of(TOP + k * T, T), T)
            for j in range(own):
                here = pl.ds(j * L, L)
                vel[0, c, at, here] = uu[c, j, at, :]
                vel[1, c, at, here] = vv[c, j, at, :]
                p, m = sp_p[c, j, at, :], sp_m[c, j, at, :]
                st[0, c, at, here] = 0.5 * (p + m) - STRENGTH * h[c, at, here]
                st[1, c, at, here] = 0.5 * (p - m)
                st[2, c, at, here] = 0.5 * sp_s[c, j, at, :]
            return 0

        lax.fori_loop(0, rows // T, out_chunk, 0, unroll=4)
        outs = [
            pltpu.make_async_copy(
                vel.at[:, c, TOP:end, :], vel_out.at[:, c], out_sem.at[2 * phase]
            ),
            pltpu.make_async_copy(
                st.at[:, c, TOP:end, :], stress_out.at[:, c], out_sem.at[2 * phase + 1]
            ),
        ]
        for copy in outs:
            copy.start()
        return outs, fcols

    def back_copies(phase, c, source, target):
        at = pl.ds(pl.multiple_of(TOP + source * rows, T), rows)
        parts = (
            (sp.at[c, :, 0:rows, :], forcing.at[:, at, :]),
            (sp.at[c, :, rows : rows + T, :], extra.at[source]),
        )
        return [
            pltpu.make_async_remote_copy(
                src_ref=src,
                dst_ref=dst,
                send_sem=back_send.at[2 * phase + i],
                recv_sem=back_recv.at[source, i],
                device_id=(target, ti),
                device_id_type=MESH,
            )
            for i, (src, dst) in enumerate(parts)
        ]

    def edge_copies():
        top, bottom = groups - 1, 0
        parts = (
            (top, 1, sp.at[0, :, rows - T : rows, :], forcing.at[:, TOP - T : TOP, :]),
            (top, 1, sp.at[0, :, rows : rows + T, :], extra.at[0]),
            (bottom, groups - 2, sp.at[1, :, 0:T, :], forcing.at[:, oend : oend + T, :]),
        )
        return [
            (
                source,
                target,
                pltpu.make_async_remote_copy(
                    src_ref=src,
                    dst_ref=dst,
                    send_sem=edge_send.at[i],
                    recv_sem=edge_recv.at[i],
                    device_id=(target, ti),
                    device_id_type=MESH,
                ),
            )
            for i, (source, target, src, dst) in enumerate(parts)
        ]

    outs_a, fcols_a = ice_cap(0)
    outs_b, fcols_b = ice_cap(1)

    def carry_over(row, source):
        for j in range(span):
            at = (j, slice(row, row + 1), slice(None))
            forcing[at] = forcing[at] - extra[source, j, T - 1 : T, :]

    for cap, home in enumerate(homes):

        @pl.when(gi == home)
        def _():
            for source in range(groups):
                if source != home:
                    phase = (source + cap) % 2
                    for copy in back_copies(phase, cap, source, source):
                        copy.wait_recv()
            for source in range(groups):
                carry_over(TOP + (source + 1) * rows, source)

    for i, (source, target, copy) in enumerate(edge_copies()):
        pl.when(gi == target)(copy.wait_recv)
        if i == 1:
            pl.when(gi == target)(lambda: carry_over(TOP, 0))

    zero = jnp.zeros((T, L), F32)

    def fold(first, second):
        total = first[0] * second[0]
        for j in range(1, own):
            total = total + first[j] * second[j]
        return total

    def first_chunk(k):
        at = chunk(k)
        r, z = [], []
        for j in range(span):
            depth = g[j, at, :]
            r.append(r0[j, at, :] + jnp.where(depth > 0.0, forcing[j, at, :], 0.0))
            z.append(r[j] * inv[j, at, :])
            v0[j, at, :] = z[j]
            w0[j, at, :] = depth * z[j]
        return fold(r, z)

    first_chunk(0)
    first_chunk(ochunks - 1)
    m0 = lax.fori_loop(1, ochunks - 1, lambda k, s: s + first_chunk(k), zero, unroll=4)

    def power(w_from, v_to, w_to):
        def body(k, turns):
            at = chunk(k)
            near = around(w_from, k, *turns)
            w_here = [w_from[j, at, :] for j in range(own)]
            w_next = []
            for j in range(span):
                v = gd[j, at, :] * near[j]
                w = g[j, at, :] * v
                if j < own:
                    v_to[j, at, :] = v
                w_to[j, at, :] = w
                w_next.append(w)
            return fold(w_here, near), fold(w_next, near)

        body(0, turned(w_from, 0))
        body(ochunks - 1, turned(w_from, ochunks - 1))

        def step(k, carry):
            turns, s0, s1 = carry
            ahead = turned(w_from, k + 1)
            a, b = body(k, turns)
            return ahead, s0 + a, s1 + b

        carry = (turned(w_from, 1), zero, zero)
        _, s0, s1 = lax.fori_loop(1, ochunks - 1, step, carry, unroll=8)
        return s0, s1

    m1, m2 = power(w0, v1, w1)
    m3, m4 = power(w1, v2, w2)

    def last_step(k, carry):
        turns, s = carry
        ahead = turned(w2, k + 1)
        near = around(w2, k, *turns)
        return ahead, s + fold([w2[j, chunk(k), :] for j in range(own)], near)

    _, m5 = lax.fori_loop(1, ochunks - 1, last_step, (turned(w2, 1), zero), unroll=8)

    row = lax.broadcasted_iota(jnp.int32, (T, L), 0)
    moments = zero
    for k, m in enumerate((m0, m1, m2, m3, m4, m5)):
        moments = jnp.where(row == k, jnp.sum(m, axis=0, keepdims=True), moments)

    def all_reduce(value, src, dst, send, recv, index, count, device):
        src[...] = value
        for d in range(1, count):
            pltpu.make_async_remote_copy(
                src_ref=src,
                dst_ref=dst.at[d],
                send_sem=send.at[d],
                recv_sem=recv.at[d],
                device_id=device(lax.rem(index + d, count)),
                device_id_type=MESH,
            ).start()
        for d in range(1, count):
            copy = pltpu.make_async_remote_copy(
                src_ref=src,
                dst_ref=dst.at[d],
                send_sem=send.at[d],
                recv_sem=recv.at[d],
                device_id=device(lax.rem(index + d, count)),
                device_id_type=MESH,
            )
            copy.wait()
        for d in range(1, count):
            value = value + dst[d]
        return value

    moments = all_reduce(
        moments, red_s, red_r, red_send, red_recv, ti, tiles, lambda k: (gi, k)
    )
    moments = all_reduce(
        moments, red2_s, red2_r, red2_send, red2_recv, gi, groups, lambda k: (k, ti)
    )
    total = jnp.sum(moments, axis=1, keepdims=True)
    nu = [total[k : k + 1, :] for k in range(6)]
    a = [nu[k] - nu[k + 1] for k in range(5)]

    tiny = 1e-12

    def safe(value, scale):
        ok = value > tiny * scale
        return jnp.where(ok, 1.0 / jnp.where(ok, value, 1.0), 0.0)

    i0 = safe(a[0], 0.0 * a[0])
    l10, l20 = a[1] * i0, a[2] * i0
    d1 = a[2] - l10 * a[1]
    i1 = safe(d1, a[2])
    e21 = a[3] - l20 * a[1]
    l21 = e21 * i1
    d2 = a[4] - l20 * a[2] - l21 * e21
    i2 = safe(d2, a[4])
    y0 = nu[0]
    y1 = nu[1] - l10 * y0
    y2 = nu[2] - l20 * y0 - l21 * y1
    c2 = y2 * i2
    c1 = y1 * i1 - l21 * c2
    c0 = y0 * i0 - l10 * c1 - l20 * c2

    def final_chunk(k, _):
        at = pl.ds(pl.multiple_of(TOP + k * T, T), T)
        for j in range(own):
            xn[at, pl.ds(j * L, L)] = x[j, at, :] + (
                c0 * v0[j, at, :] + (c1 * v1[j, at, :] + c2 * v2[j, at, :])
            )
        return 0

    lax.fori_loop(0, orows // T, final_chunk, 0, unroll=4)
    last = pltpu.make_async_copy(xn.at[TOP:oend, :], ssh_out, out_sem.at[4])
    last.start()

    for way, copy in early + late + orow:
        pl.when(edge(way, gi, groups)[0])(copy.wait_send)
    for way, copy in ocols + icols + fcols_a + fcols_b:
        pl.when(edge(way, ti, tiles)[0])(copy.wait_send)
    for cap, home in enumerate(homes):

        @pl.when(gi == home)
        def _():
            for target in range(groups):
                if target != home:
                    for piece in range(3):
                        flow_copy(cap, target, piece).wait_send()

    for phase in range(2):
        c = lax.rem(gi + phase, 2)

        @pl.when(gi != c * (groups - 1))
        def _():
            for copy in back_copies(phase, c, gi, c * (groups - 1)):
                copy.wait_send()

    for source, target, copy in edge_copies():
        pl.when(gi == source)(copy.wait_send)
    for copy in outs_a + outs_b:
        copy.wait()
    last.wait()


def deliver(*refs):
    half = len(refs) // 2
    for src, dst in zip(refs[:half], refs[half:]):
        dst[...] = src[...]


def step(groups, tiles, *args):
    base_rhs, thick, ice_vel, ice_stress = args[0], args[5], args[7], args[8]
    orows, cols = base_rhs.shape
    rows = thick.shape[1]
    irows = rows + 2 * TOP
    erows = orows + 2 * TOP
    span = cols // L + 1
    any_spec = pl.BlockSpec(memory_space=pl.ANY)
    hbm = pl.BlockSpec(memory_space=pltpu.HBM)
    vmem = pl.BlockSpec(memory_space=pltpu.VMEM)
    dma = pltpu.SemaphoreType.DMA
    ice = pltpu.VMEM((2, span, irows + PAD, L), F32)
    ocean = pltpu.VMEM((span, erows + PAD, L), F32)
    plain = pltpu.VMEM((erows, cols), F32)
    results = pl.pallas_call(
        functools.partial(kernel, groups, tiles),
        out_shape=(
            jax.ShapeDtypeStruct(base_rhs.shape, F32),
            jax.ShapeDtypeStruct(ice_vel.shape, F32),
            jax.ShapeDtypeStruct(ice_stress.shape, F32),
        ),
        in_specs=[hbm] * 4 + [vmem, hbm, vmem] + [hbm] * 3,
        out_specs=(any_spec,) * 3,
        scratch_shapes=[
            pltpu.VMEM((2, 2, irows, cols), F32),
            pltpu.VMEM((3, 2, irows, cols), F32),
            pltpu.VMEM((2, 2, irows, cols), F32),
            pltpu.VMEM((2, 2, irows, cols), F32),
            pltpu.VMEM((2, irows, cols), F32),
            plain,
            plain,
            plain,
        ]
        + [ice] * 8
        + [
            pltpu.VMEM((2, 2, span, irows + PAD, L), F32),
            pltpu.VMEM((2, 2, irows, L), F32),
        ]
        + [ocean] * 13
        + [
            pltpu.VMEM((orows // BS, cols), F32),
            pltpu.VMEM((2, rows // BS, cols), F32),
            pltpu.VMEM((2, 2, rows + 2 * T, L), F32),
            pltpu.VMEM((2, 2, rows + 2 * T, L), F32),
            pltpu.VMEM((2, 2, rows + 2 * T, L), F32),
            pltpu.VMEM((2, 2, rows + 2 * T, L), F32),
            pltpu.VMEM((2, orows + 2 * T, L), F32),
            pltpu.VMEM((2, orows + 2 * T, L), F32),
            pltpu.VMEM((2, span, rows + T, L), F32),
            pltpu.VMEM((groups, span, T, L), F32),
            pltpu.VMEM((T, L), F32),
            pltpu.VMEM((tiles, T, L), F32),
            pltpu.VMEM((T, L), F32),
            pltpu.VMEM((groups, T, L), F32),
            dma((7,)),
            dma((3 * groups,)),
            dma((6,)),
            dma((14,)),
            dma((14,)),
            dma((8,)),
            dma((8,)),
            dma((4,)),
            dma((groups, 2)),
            dma((3,)),
            dma((3,)),
            dma((tiles,)),
            dma((tiles,)),
            dma((groups,)),
            dma((groups,)),
            dma((5,)),
        ],
        compiler_params=pltpu.CompilerParams(
            collective_id=0, has_side_effects=True, vmem_limit_bytes=67_043_328
        ),
    )(*args)
    return pl.pallas_call(
        deliver,
        out_shape=tuple(jax.ShapeDtypeStruct(r.shape, F32) for r in results),
        in_specs=[vmem] * 3,
        out_specs=(vmem,) * 3,
    )(*results)


def solution(mesh):
    grid = P("grp", "tile")
    plane = P(None, "grp", "tile")
    stack = P(None, None, "grp", "tile")
    return jax.shard_map(
        functools.partial(step, mesh.shape["grp"], mesh.shape["tile"]),
        mesh=mesh,
        in_specs=(grid, grid, grid, plane, grid, plane, plane, stack, stack, stack),
        out_specs=(grid, stack, stack),
        check_vma=False,
    )
```

time: 69.3 us -> 62.6 us (0.903)
  Pallas kernels: 68.3 us -> 61.6 us
    pallas_call x1, Pallas kernels: 65.6 us -> 58.9 us  [step(): pl.pallas_call(functools.partial(kernel, groups, tiles), out_shape=(jax.S...]
where the time goes in v1:
time: 62.6 us; the launch traced here: 62.3 us
  Pallas kernels  61.6 us (98%)
  between operations  0.64 us (1%)
    pallas_call x1, Pallas kernels, step(): pl.pallas_call(functools.partial(kernel, groups, tiles), out_shape=(jax.S...  58.9 us
    pallas_call x1, Pallas kernels, step(): pl.pallas_call(deliver, out_shape=tuple((jax.ShapeDtypeStruct(r.shape, F3...  2.71 us

profile of v1, /device:TPU:0, one launch (start us, length us, event | category | flops | bytes accessed | tf_op | source)
XLA Modules:
  0.0 62.3 jit_solution(10440983156632563712)
XLA Ops:
  0.6 58.9 %shard_map.121 = (f32[256,512]{1,0:T(8,128)}, f32[2,2,64,512]{3,2,1,0:T(8,128)}, f32[3,2,64,512]{3,2,1,0:T(8,128)}) custom-call(f32[256,512]{1,0:T(8,128)} %base_in.1, f32[256,512]{1,0:T(8,128)} %depth_in.1, f32[256,512]{1,0:T(8,128)} %ssh_in.1, f32[2,256,512]{2,1,0:T(8,128)} %cur_in.1, s32[32,64]{1,0:T(8,128)} %land_ref.1, f32[2,64,512]{2,1,0:T(8,128)} %thick_in.1, ...), custom_call_target="tpu_custom_call" | custom-call | tf_op jit(solution)/shard_map/pallas_call | solution.py:912
  59.5 2.7 %shard_map.122 = (f32[256,512]{1,0:T(8,128)}, f32[2,2,64,512]{3,2,1,0:T(8,128)}, f32[3,2,64,512]{3,2,1,0:T(8,128)}) custom-call(f32[256,512]{1,0:T(8,128)} %get-tuple-element.6.refs_0_, f32[2,2,64,512]{3,2,1,0:T(8,128)} %get-tuple-element.7.refs_1_, f32[3,2,64,512]{3,2,1,0:T(8,128)} %get-tuple-element.8.refs_2_), custom_call_target="tpu_custom_call" | custom-call | tf_op jit(solution)/shard_map/pallas_call | solution.py:973

commit v2 on v1

--- a/solution.py
+++ b/solution.py
@@ -232,43 +232,68 @@
             device_id_type=MESH,
         )
 
-    def row_copies(which):
+    def row_copy(k, way, src, dst, first, after, ends):
+        count, last = ends
+        from_row = first + count - T if way == 0 else first
+        to_row = after - T if way == 0 else last
+        return (
+            way,
+            pltpu.make_async_remote_copy(
+                src_ref=src(pl.ds(from_row, T)),
+                dst_ref=dst(pl.ds(to_row, T)),
+                send_sem=row_send.at[2 * k + way],
+                recv_sem=row_recv.at[2 * k + way],
+                device_id=(lax.rem(gi + (1 if way == 0 else groups - 1), groups), ti),
+                device_id_type=MESH,
+            ),
+        )
+
+    def ice_rows(stage):
+        c = lax.rem(gi + 1 + stage, 2)
+        fields = ((vel_in, vel), (stress_in, st), (wind_in, wind))
         out = []
-        fields = (
-            (vel_in, vel, rows, end),
-            (stress_in, st, rows, end),
-            (wind_in, wind, rows, end),
-            (ssh_in, xn, orows, oend),
-            (base_in, bn, orows, oend),
-            (h, h, None, end),
-            (gn, gn, None, oend),
-        )
-        for k, (src, dst, length, last) in enumerate(fields):
-            if k not in which:
-                continue
-            origin = TOP if length is None else 0
-            count = (last - TOP) if length is None else length
-            lead = (slice(None),) * (len(src.shape) - 2)
+        for k, (src, dst) in enumerate(fields):
             for way in range(2):
-                from_row = origin + count - T if way == 0 else origin
-                to_row = TOP - T if way == 0 else last
                 out.append(
-                    (
+                    row_copy(
+                        4 * stage + k,
                         way,
-                        pltpu.make_async_remote_copy(
-                            src_ref=src.at[lead + (slice(from_row, from_row + T), slice(0, cols))],
-                            dst_ref=dst.at[lead + (slice(to_row, to_row + T), slice(0, cols))],
-                            send_sem=row_send.at[2 * k + way],
-                            recv_sem=row_recv.at[2 * k + way],
-                            device_id=(
-                                lax.rem(gi + (1 if way == 0 else groups - 1), groups),
-                                ti,
-                            ),
-                            device_id_type=MESH,
-                        ),
+                        lambda at, src=src: src.at[:, c, at, :],
+                        lambda at, dst=dst: dst.at[:, c, at, :],
+                        0,
+                        TOP,
+                        (rows, end),
                     )
                 )
+        for way in range(2):
+            out.append(
+                row_copy(
+                    4 * stage + 3,
+                    way,
+                    lambda at: h.at[c, at, :],
+                    lambda at: h.at[c, at, :],
+                    TOP,
+                    TOP,
+                    (rows, end),
+                )
+            )
         return out
+
+    def ocean_rows():
+        fields = ((ssh_in, xn, 0), (base_in, bn, 0), (gn, gn, TOP))
+        return [
+            row_copy(
+                8 + k,
+                way,
+                lambda at, src=src: src.at[at, :],
+                lambda at, dst=dst: dst.at[at, :],
+                first,
+                TOP,
+                (orows, oend),
+            )
+            for k, (src, dst, first) in enumerate(fields)
+            for way in range(2)
+        ]
 
     def edge(way, index, count):
         sends = index < count - 1 if way == 0 else index > 0
@@ -282,9 +307,6 @@
     def receive_all(copies, index, count):
         for way, copy in copies:
             pl.when(edge(way, index, count)[1])(copy.wait_recv)
-
-    early = row_copies((0, 1, 2))
-    start_all(early, gi, groups)
 
     for cap, home in enumerate(homes):
 
@@ -302,19 +324,9 @@
         return 0
 
     lax.fori_loop(0, rows // T, cover_chunk, 0, unroll=4)
-    late = row_copies((5,))
-    start_all(late, gi, groups)
-
-    load_depth.wait()
-
-    def wet_chunk(k, _):
-        at = (pl.ds(pl.multiple_of(TOP + k * T, T), T), slice(None))
-        gn[at] = gn[at] * wet[pl.ds(k, 1), :]
-        return 0
-
-    lax.fori_loop(0, orows // T, wet_chunk, 0, unroll=4)
-    orow = row_copies((3, 4, 6))
-    start_all(orow, gi, groups)
+    irow = [ice_rows(stage) for stage in range(2)]
+    start_all(irow[0], gi, groups)
+    start_all(irow[1], gi, groups)
 
     for cap, home in enumerate(homes):
 
@@ -325,12 +337,22 @@
                 for piece in range(3):
                     flow_copy(cap, target, piece).start()
 
+    load_depth.wait()
+
+    def wet_chunk(k, _):
+        at = (pl.ds(pl.multiple_of(TOP + k * T, T), T), slice(None))
+        gn[at] = gn[at] * wet[pl.ds(k, 1), :]
+        return 0
+
+    lax.fori_loop(0, orows // T, wet_chunk, 0, unroll=4)
+    orow = ocean_rows()
+    start_all(orow, gi, groups)
+
     load_vel.wait()
     load_st.wait()
     load_wind.wait()
     load_x.wait()
     load_b.wait()
-    receive_all(early + late, gi, groups)
 
     lane = lanes(T, L)
 
@@ -387,30 +409,31 @@
     def chunk0(k):
         return pl.ds(pl.multiple_of(k * T, T), T)
 
-    def pack_chunk(k, _):
-        for c in range(2):
+    def pack(stage):
+        c = lax.rem(gi + stage, 2)
+
+        def body(k, _):
             after, before = packed(ends(ice_fields(c), chunk(k)))
             pack_s[0, c, chunk0(k), :] = after
             pack_s[1, c, chunk0(k), :] = before
-        return 0
-
-    lax.fori_loop(0, ichunks, pack_chunk, 0, unroll=5)
-    icols = col_copies(lambda way: pack_s.at[way], lambda way: pack_r.at[way], 0)
-    start_all(icols, ti, tiles)
-
-    receive_all(orow, gi, groups)
-
-    def opack_chunk(k, _):
-        after, before = packed(ends((gn, xn, bn), chunk(k)))
-        opack_s[0, chunk0(k), :] = after
-        opack_s[1, chunk0(k), :] = before
-        return 0
-
-    lax.fori_loop(0, ochunks, opack_chunk, 0, unroll=17 if ochunks % 17 == 0 else 1)
-    ocols = col_copies(lambda way: opack_s.at[way], lambda way: opack_r.at[way], 2)
-    start_all(ocols, ti, tiles)
-
-    receive_all(icols, ti, tiles)
+            return 0
+
+        lax.fori_loop(0, ichunks, body, 0, unroll=ichunks)
+        icols = col_copies(lambda way: pack_s.at[way, c], lambda way: pack_r.at[way, c], 4 * stage)
+        start_all(icols, ti, tiles)
+        return icols
+
+    def pack_ocean():
+        def body(k, _):
+            after, before = packed(ends((gn, xn, bn), chunk(k)))
+            opack_s[0, chunk0(k), :] = after
+            opack_s[1, chunk0(k), :] = before
+            return 0
+
+        lax.fori_loop(0, ochunks, body, 0, unroll=17 if ochunks % 17 == 0 else 1)
+        ocols = col_copies(lambda way: opack_s.at[way], lambda way: opack_r.at[way], 8)
+        start_all(ocols, ti, tiles)
+        return ocols
 
     def prep(c):
         def body(k, thick_up):
@@ -440,12 +463,7 @@
             return tuple(thicks)
 
         zero = jnp.zeros((T, L), F32)
-        lax.fori_loop(0, ichunks, body, (zero,) * span, unroll=2)
-
-    prep(0)
-    prep(1)
-
-    receive_all(ocols, ti, tiles)
+        lax.fori_loop(0, ichunks, body, (zero,) * span, unroll=ichunks // 2)
 
     def ocean_chunk(k, _):
         at = chunk(k)
@@ -459,8 +477,6 @@
             r0[j, at, :] = jnp.where(depth > 0.0, base, 0.0)
         return 0
 
-    lax.fori_loop(0, ochunks, ocean_chunk, 0, unroll=2)
-
     def around(ref, k, lefts, rights):
         r = T + k * T
         up, down = pl.ds(r - 1, T), pl.ds(r + 1, T)
@@ -473,10 +489,11 @@
         values = [ref[j, chunk(k), :] for j in range(span)]
         return turn_left(values), turn_right(values)
 
-    def pre_chunk(k, _):
+    def pre_chunk(k, carry):
         at = chunk(k)
-        g_near = around(g, k, *turned(g, k))
-        near = around(gx, k, *turned(gx, k))
+        ahead = (turned(g, k + 1), turned(gx, k + 1))
+        g_near = around(g, k, *carry[0])
+        near = around(gx, k, *carry[1])
         for j in range(span):
             depth = g[j, at, :]
             diag = DAMP + depth * g_near[j]
@@ -484,13 +501,18 @@
             r0[j, at, :] = r0[j, at, :] - diag * x[j, at, :] + depth * near[j]
             inv[j, at, :] = inverse
             gd[j, at, :] = depth * inverse
-        return 0
-
-    lax.fori_loop(0, ochunks, pre_chunk, 0, unroll=2)
+        return ahead
+
+    def prepare_ocean():
+        steps = 17 if ochunks % 17 == 0 else 2
+        lax.fori_loop(0, ochunks, ocean_chunk, 0, unroll=steps)
+        lax.fori_loop(0, ochunks, pre_chunk, (turned(g, 0), turned(gx, 0)), unroll=steps)
 
     def ice_cap(phase):
         c = lax.rem(gi + phase, 2)
 
+        receive_all(irow[phase], gi, groups)
+        icols = pack(phase)
 
         def flow_wait(which):
             for target in range(groups):
@@ -515,9 +537,11 @@
 
         lax.fori_loop(0, ichunks, fpack_chunk, 0, unroll=ichunks)
         fcols = col_copies(
-            lambda way: fpack_s.at[way, c], lambda way: fpack_r.at[way, c], 4 + 2 * phase
+            lambda way: fpack_s.at[way, c], lambda way: fpack_r.at[way, c], 4 * phase + 2
         )
         start_all(fcols, ti, tiles)
+        receive_all(icols, ti, tiles)
+        prep(c)
         flow_wait((2,))
         receive_all(fcols, ti, tiles)
 
@@ -658,7 +682,7 @@
         ]
         for copy in outs:
             copy.start()
-        return outs, fcols
+        return outs, icols + fcols
 
     def back_copies(phase, c, source, target):
         at = pl.ds(pl.multiple_of(TOP + source * rows, T), rows)
@@ -701,8 +725,13 @@
             for i, (source, target, src, dst) in enumerate(parts)
         ]
 
-    outs_a, fcols_a = ice_cap(0)
-    outs_b, fcols_b = ice_cap(1)
+    outs_a, cols_a = ice_cap(0)
+    outs_b, cols_b = ice_cap(1)
+
+    receive_all(orow, gi, groups)
+    ocols = pack_ocean()
+    receive_all(ocols, ti, tiles)
+    prepare_ocean()
 
     def carry_over(row, source):
         for j in range(span):
@@ -861,9 +890,9 @@
     last = pltpu.make_async_copy(xn.at[TOP:oend, :], ssh_out, out_sem.at[4])
     last.start()
 
-    for way, copy in early + late + orow:
+    for way, copy in irow[0] + irow[1] + orow:
         pl.when(edge(way, gi, groups)[0])(copy.wait_send)
-    for way, copy in ocols + icols + fcols_a + fcols_b:
+    for way, copy in ocols + cols_a + cols_b:
         pl.when(edge(way, ti, tiles)[0])(copy.wait_send)
     for cap, home in enumerate(homes):
 
@@ -952,10 +981,10 @@
             dma((7,)),
             dma((3 * groups,)),
             dma((6,)),
-            dma((14,)),
-            dma((14,)),
-            dma((8,)),
-            dma((8,)),
+            dma((22,)),
+            dma((22,)),
+            dma((10,)),
+            dma((10,)),
             dma((4,)),
             dma((groups, 2)),
             dma((3,)),

time: 62.6 us -> 53.2 us (0.85)
  Pallas kernels: 61.6 us -> 52.3 us
    pallas_call x1, Pallas kernels: 58.9 us -> 49.6 us  [step(): pl.pallas_call(functools.partial(kernel, groups, tiles), out_shape=(jax.S...]
where the time goes in v2:
time: 53.2 us; the launch traced here: 52.9 us
  Pallas kernels  52.3 us (98%)
  between operations  0.64 us (1%)
    pallas_call x1, Pallas kernels, step(): pl.pallas_call(functools.partial(kernel, groups, tiles), out_shape=(jax.S...  49.6 us
    pallas_call x1, Pallas kernels, step(): pl.pallas_call(deliver, out_shape=tuple((jax.ShapeDtypeStruct(r.shape, F3...  2.71 us

profile of v2, /device:TPU:0, one launch (start us, length us, event | category | flops | bytes accessed | tf_op | source)
XLA Modules:
  0.0 52.9 jit_solution(18430322673268044)
XLA Ops:
  0.6 49.6 %shard_map.121 = (f32[256,512]{1,0:T(8,128)}, f32[2,2,64,512]{3,2,1,0:T(8,128)}, f32[3,2,64,512]{3,2,1,0:T(8,128)}) custom-call(f32[256,512]{1,0:T(8,128)} %base_in.1, f32[256,512]{1,0:T(8,128)} %depth_in.1, f32[256,512]{1,0:T(8,128)} %ssh_in.1, f32[2,256,512]{2,1,0:T(8,128)} %cur_in.1, s32[32,64]{1,0:T(8,128)} %land_ref.1, f32[2,64,512]{2,1,0:T(8,128)} %thick_in.1, ...), custom_call_target="tpu_custom_call" | custom-call | tf_op jit(solution)/shard_map/pallas_call | solution.py:941
  50.2 2.7 %shard_map.122 = (f32[256,512]{1,0:T(8,128)}, f32[2,2,64,512]{3,2,1,0:T(8,128)}, f32[3,2,64,512]{3,2,1,0:T(8,128)}) custom-call(f32[256,512]{1,0:T(8,128)} %get-tuple-element.6.refs_0_, f32[2,2,64,512]{3,2,1,0:T(8,128)} %get-tuple-element.7.refs_1_, f32[3,2,64,512]{3,2,1,0:T(8,128)} %get-tuple-element.8.refs_2_), custom_call_target="tpu_custom_call" | custom-call | tf_op jit(solution)/shard_map/pallas_call | solution.py:1002

commit v3 on v2

--- a/solution.py
+++ b/solution.py
@@ -72,15 +72,17 @@
     depth_in,
     ssh_in,
     cur_in,
-    land_ref,
+    land_in,
     thick_in,
-    ice_ref,
+    ice_in,
     vel_in,
     stress_in,
     wind_in,
     ssh_out,
     vel_out,
     stress_out,
+    land_ref,
+    ice_ref,
     vel,
     st,
     wind,
@@ -121,7 +123,8 @@
     opack_s,
     opack_r,
     sp,
-    extra,
+    trim_s,
+    trim_r,
     red_s,
     red_r,
     red2_s,
@@ -141,7 +144,6 @@
     red_recv,
     red2_send,
     red2_recv,
-    out_sem,
 ):
     gi = lax.axis_index("grp")
     ti = lax.axis_index("tile")
@@ -154,33 +156,6 @@
     ichunks = rows // T + 2
     ochunks = orows // T + 2
 
-    loads = []
-
-    def load(src, dst):
-        copy = pltpu.make_async_copy(src, dst, load_sem.at[len(loads)])
-        copy.start()
-        loads.append(copy)
-        return copy
-
-    load_thick = load(thick_in, h.at[:, TOP:end, :])
-    load_depth = load(depth_in, gn.at[TOP:oend, :])
-    load_x = load(ssh_in, xn.at[TOP:oend, :])
-    load_b = load(base_in, bn.at[TOP:oend, :])
-    load_vel = load(vel_in, vel.at[:, :, TOP:end, :])
-    load_st = load(stress_in, st.at[:, :, TOP:end, :])
-    load_wind = load(wind_in, wind.at[:, :, TOP:end, :])
-
-    def clear(ref, *spans):
-        for lo, hi in spans:
-            ref[..., lo:hi, :] = jnp.zeros(ref.shape[:-2] + (hi - lo, ref.shape[-1]), F32)
-
-    for ref in (vel, st, wind, flow, h):
-        clear(ref, (T, TOP), (end, end + T))
-    for ref in (gn, xn, bn):
-        clear(ref, (T, TOP), (oend, oend + T))
-    for ref in (pack_r, fpack_r, opack_r, forcing):
-        ref[...] = jnp.zeros_like(ref)
-
     barrier = pltpu.get_barrier_semaphore()
     for d in range(1, groups):
         pl.semaphore_signal(
@@ -191,10 +166,58 @@
             barrier, inc=1, device_id=(gi, lax.rem(ti + d, tiles)), device_id_type=MESH
         )
 
+    loads = []
+
+    def load(src, dst):
+        copy = pltpu.make_async_copy(src, dst, load_sem.at[len(loads)])
+        copy.start()
+        loads.append(copy)
+        return copy
+
+    load_land = load(land_in, land_ref)
+    load_ice = load(ice_in, ice_ref)
+    load_thick = load(thick_in, h.at[:, TOP:end, :])
+    load_vel = load(vel_in, vel.at[:, :, TOP:end, :])
+    load_st = load(stress_in, st.at[:, :, TOP:end, :])
+    load_wind = load(wind_in, wind.at[:, :, TOP:end, :])
+    load_depth = load(depth_in, gn.at[TOP:oend, :])
+    load_x = load(ssh_in, xn.at[TOP:oend, :])
+    load_b = load(base_in, bn.at[TOP:oend, :])
+
+    def clear(ref, *spans):
+        for lo, hi in spans:
+            ref[..., lo:hi, :] = jnp.zeros(ref.shape[:-2] + (hi - lo, ref.shape[-1]), F32)
+
+    for outer, before in ((gi == 0, True), (gi == groups - 1, False)):
+
+        @pl.when(outer)
+        def _():
+            for ref in (vel, st, wind, flow, h):
+                clear(ref, (T, TOP) if before else (end, end + T))
+            for ref in (gn, xn, bn):
+                clear(ref, (T, TOP) if before else (oend, oend + T))
+            clear(forcing, (T, TOP), (oend, oend + T))
+
+    for outer, way in ((ti == 0, 0), (ti == tiles - 1, 1)):
+
+        @pl.when(outer)
+        def _():
+            for ref in (pack_r, fpack_r, opack_r):
+                ref[way] = jnp.zeros(ref.shape[1:], F32)
+
+    @pl.when((gi > 0) & (gi < groups - 1))
+    def _():
+        clear(forcing, (TOP, oend))
+        pl.when(gi != 1)(lambda: clear(forcing, (T, TOP)))
+        pl.when(gi != groups - 2)(lambda: clear(forcing, (oend, oend + T)))
+
     for ref in (uu, vv, sp_p, sp_m, sp_s):
         clear(ref, (0, T), (end + T, end + 2 * T))
     for ref in (g, gx, w0, w1, w2):
         clear(ref, (0, T), (oend + T, oend + 2 * T))
+
+    load_land.wait()
+    load_ice.wait()
 
     def blocks(ref, out, count):
         width = ref.shape[-1]
@@ -214,23 +237,30 @@
     homes = (0, groups - 1)
     pieces = ((0, L), (cols - L, cols), (L, cols - L))
 
-    def flow_copy(cap, target, piece):
+    def flow_span(target):
         lo = max(0, rows * target - T)
         hi = min(rows * groups, rows * target + rows + T)
-        start = TOP + lo - rows * target
+        return lo, hi, TOP + lo - rows * target
+
+    def flow_copy(cap, target, piece):
+        lo, hi, start = flow_span(target)
         first, last = pieces[piece]
         src = cur_in.at[:, lo:hi, first:last]
         dst = flow.at[:, cap, start : start + hi - lo, first:last]
+        recv = flow_recv.at[2 * cap + piece // 2]
         if target == homes[cap]:
-            return pltpu.make_async_copy(src, dst, flow_recv.at[3 * cap + piece])
+            return pltpu.make_async_copy(src, dst, recv)
         return pltpu.make_async_remote_copy(
             src_ref=src,
             dst_ref=dst,
-            send_sem=flow_send.at[3 * target + piece],
-            recv_sem=flow_recv.at[3 * cap + piece],
+            send_sem=flow_send,
+            recv_sem=recv,
             device_id=(target, ti),
             device_id_type=MESH,
         )
+
+    def take(ref, sem):
+        pltpu.make_async_copy(ref, ref, sem).wait()
 
     def row_copy(k, way, src, dst, first, after, ends):
         count, last = ends
@@ -241,7 +271,7 @@
             pltpu.make_async_remote_copy(
                 src_ref=src(pl.ds(from_row, T)),
                 dst_ref=dst(pl.ds(to_row, T)),
-                send_sem=row_send.at[2 * k + way],
+                send_sem=row_send.at[way],
                 recv_sem=row_recv.at[2 * k + way],
                 device_id=(lax.rem(gi + (1 if way == 0 else groups - 1), groups), ti),
                 device_id_type=MESH,
@@ -250,17 +280,16 @@
 
     def ice_rows(stage):
         c = lax.rem(gi + 1 + stage, 2)
-        fields = ((vel_in, vel), (stress_in, st), (wind_in, wind))
         out = []
-        for k, (src, dst) in enumerate(fields):
+        for ref in (vel, st, wind):
             for way in range(2):
                 out.append(
                     row_copy(
-                        4 * stage + k,
+                        stage,
                         way,
-                        lambda at, src=src: src.at[:, c, at, :],
-                        lambda at, dst=dst: dst.at[:, c, at, :],
-                        0,
+                        lambda at, ref=ref: ref.at[:, c, at, :],
+                        lambda at, ref=ref: ref.at[:, c, at, :],
+                        TOP,
                         TOP,
                         (rows, end),
                     )
@@ -268,7 +297,7 @@
         for way in range(2):
             out.append(
                 row_copy(
-                    4 * stage + 3,
+                    stage,
                     way,
                     lambda at: h.at[c, at, :],
                     lambda at: h.at[c, at, :],
@@ -280,18 +309,17 @@
         return out
 
     def ocean_rows():
-        fields = ((ssh_in, xn, 0), (base_in, bn, 0), (gn, gn, TOP))
         return [
             row_copy(
-                8 + k,
+                2,
                 way,
-                lambda at, src=src: src.at[at, :],
-                lambda at, dst=dst: dst.at[at, :],
-                first,
+                lambda at, ref=ref: ref.at[at, :],
+                lambda at, ref=ref: ref.at[at, :],
+                TOP,
                 TOP,
                 (orows, oend),
             )
-            for k, (src, dst, first) in enumerate(fields)
+            for ref in (xn, bn, gn)
             for way in range(2)
         ]
 
@@ -307,6 +335,12 @@
     def receive_all(copies, index, count):
         for way, copy in copies:
             pl.when(edge(way, index, count)[1])(copy.wait_recv)
+
+    def receive_rows(k, count):
+        for way in range(2):
+            pl.when(edge(way, gi, groups)[1])(
+                lambda: take(gn.at[0:count, :], row_recv.at[2 * k + way])
+            )
 
     for cap, home in enumerate(homes):
 
@@ -324,19 +358,10 @@
         return 0
 
     lax.fori_loop(0, rows // T, cover_chunk, 0, unroll=4)
-    irow = [ice_rows(stage) for stage in range(2)]
-    start_all(irow[0], gi, groups)
-    start_all(irow[1], gi, groups)
-
-    for cap, home in enumerate(homes):
-
-        @pl.when(gi == home)
-        def _():
-            order = sorted((k for k in range(groups) if k != home), key=lambda k: abs(k - home))
-            for target in order[1:] + order[:1]:
-                for piece in range(3):
-                    flow_copy(cap, target, piece).start()
-
+    load_vel.wait()
+    load_st.wait()
+    load_wind.wait()
+    start_all(ice_rows(0), gi, groups)
     load_depth.wait()
 
     def wet_chunk(k, _):
@@ -345,14 +370,23 @@
         return 0
 
     lax.fori_loop(0, orows // T, wet_chunk, 0, unroll=4)
-    orow = ocean_rows()
-    start_all(orow, gi, groups)
-
-    load_vel.wait()
-    load_st.wait()
-    load_wind.wait()
     load_x.wait()
     load_b.wait()
+    start_all(ocean_rows(), gi, groups)
+
+    def send_flow(which):
+        for cap, home in enumerate(homes):
+
+            @pl.when(gi == home)
+            def _():
+                order = sorted((k for k in range(groups) if k != home), key=lambda k: abs(k - home))
+                for target in which(order):
+                    for piece in range(3):
+                        flow_copy(cap, target, piece).start()
+
+    send_flow(lambda order: order[1:])
+    start_all(ice_rows(1), gi, groups)
+    send_flow(lambda order: order[:1])
 
     lane = lanes(T, L)
 
@@ -365,7 +399,7 @@
                     pltpu.make_async_remote_copy(
                         src_ref=src(way),
                         dst_ref=dst(way),
-                        send_sem=col_send.at[base + way],
+                        send_sem=col_send.at[way],
                         recv_sem=col_recv.at[base + way],
                         device_id=(gi, lax.rem(ti + (1 if way == 0 else tiles - 1), tiles)),
                         device_id_type=MESH,
@@ -435,7 +469,9 @@
         start_all(ocols, ti, tiles)
         return ocols
 
-    def prep(c):
+    def prep(phase):
+        c = lax.rem(gi + phase, 2)
+
         def body(k, thick_up):
             at = chunk(k)
             fields = ice_fields(c)
@@ -508,26 +544,19 @@
         lax.fori_loop(0, ochunks, ocean_chunk, 0, unroll=steps)
         lax.fori_loop(0, ochunks, pre_chunk, (turned(g, 0), turned(gx, 0)), unroll=steps)
 
-    def ice_cap(phase):
+    def flow_wait(phase, part):
+        for target in range(groups):
+
+            @pl.when(gi == target)
+            def _():
+                cap = (target + phase) % 2
+                lo, hi, start = flow_span(target)
+                width = 2 * L if part == 0 else cols - 2 * L
+                ref = flow.at[:, cap, start : start + hi - lo, 0:width]
+                take(ref, flow_recv.at[2 * cap + part])
+
+    def pack_flow(phase):
         c = lax.rem(gi + phase, 2)
-
-        receive_all(irow[phase], gi, groups)
-        icols = pack(phase)
-
-        def flow_wait(which):
-            for target in range(groups):
-
-                @pl.when(gi == target)
-                def _():
-                    cap = (target + phase) % 2
-                    for piece in which:
-                        copy = flow_copy(cap, target, piece)
-                        if target == homes[cap]:
-                            copy.wait()
-                        else:
-                            copy.wait_recv()
-
-        flow_wait((0, 1))
 
         def fpack_chunk(k, _):
             after, before = packed(ends((flow.at[0, c], flow.at[1, c]), chunk(k)))
@@ -540,10 +569,10 @@
             lambda way: fpack_s.at[way, c], lambda way: fpack_r.at[way, c], 4 * phase + 2
         )
         start_all(fcols, ti, tiles)
-        receive_all(icols, ti, tiles)
-        prep(c)
-        flow_wait((2,))
-        receive_all(fcols, ti, tiles)
+        return fcols
+
+    def add_flow(phase):
+        c = lax.rem(gi + phase, 2)
 
         def flow_chunk(k, _):
             at = chunk(k)
@@ -559,6 +588,9 @@
             return 0
 
         lax.fori_loop(0, ichunks, flow_chunk, 0, unroll=ichunks)
+
+    def subcycles(phase, first, last):
+        c = lax.rem(gi + phase, 2)
 
         def subcycle(n, _):
             ahead, behind = 2, 2
@@ -610,7 +642,12 @@
                     momentum(k - behind)
             return 0
 
-        lax.fori_loop(0, NSUB, subcycle, 0)
+        lax.fori_loop(first, last, subcycle, 0)
+
+    def drag(phase):
+        c = lax.rem(gi + phase, 2)
+        home = c * (groups - 1)
+        edge_lanes = L // (2 * (rows // T))
 
         def drag_chunk(k, drag_up):
             at = pl.ds(pl.multiple_of(TOP + k * T, T), T)
@@ -627,87 +664,89 @@
             beside = left(drags[1])
             for j in range(span):
                 d0 = drags[0][j]
-                d0_up = above(jnp.zeros((T, L), F32) if drag_up is None else drag_up[j], d0)
-                sp[c, j, chunk0(k), :] = (d0 - d0_up) + (drags[1][j] - beside[j])
-            return tuple(drags[0])
+                d0_up = above(drag_up[j], d0)
+                value = (d0 - d0_up) + (drags[1][j] - beside[j])
+                if j < own:
+                    sp[c, j, chunk0(k), :] = value
+                else:
+                    rim = value
+            return tuple(drags[0]), rim
 
         zero = jnp.zeros((T, L), F32)
-        last = lax.fori_loop(0, rows // T, drag_chunk, (zero,) * span, unroll=rows // T)
+        upper, rims = (zero,) * span, zero
+        for k in range(rows // T):
+            upper, rim = drag_chunk(k, upper)
+            width = 2 * edge_lanes
+            here = (lane >= width * k) & (lane < width * k + width)
+            rims = jnp.where(here, pltpu.roll(rim, (edge_lanes + width * k) % L, 1), rims)
+        trim_s[c, 0] = rims
+        row = lax.broadcasted_iota(jnp.int32, (T, L), 0)
+        last = zero
         for j in range(span):
-            sp[c, j, rows : rows + T, :] = last[j]
-
-        home = c * (groups - 1)
+            last = jnp.where(row == j, upper[j][T - 1 : T, :], last)
+        trim_s[c, 1] = last
 
         @pl.when(gi != home)
         def _():
             for copy in back_copies(phase, c, gi, home):
                 copy.start()
 
+        if phase == 1:
+            for source, target, copy in edge_copies():
+                pl.when(gi == source)(copy.start)
+
         @pl.when(gi == home)
         def _():
             row = pl.multiple_of(TOP + gi * rows, T)
-            for j in range(span):
+            for j in range(own):
 
                 def own_chunk(k, _):
                     forcing[j, pl.ds(pl.multiple_of(row + k * T, T), T), :] = sp[c, j, chunk0(k), :]
                     return 0
 
                 lax.fori_loop(0, rows // T, own_chunk, 0, unroll=rows // T)
-                extra[gi, j] = sp[c, j, rows : rows + T, :]
-
-        if phase == 1:
-            for copy in edge_copies():
-                pl.when(gi == copy[0])(copy[2].start)
+            trim_r[gi] = trim_s[c]
+
+    def output(phase):
+        c = lax.rem(gi + phase, 2)
 
         def out_chunk(k, _):
             at = pl.ds(pl.multiple_of(TOP + k * T, T), T)
+            to = chunk0(k)
             for j in range(own):
                 here = pl.ds(j * L, L)
-                vel[0, c, at, here] = uu[c, j, at, :]
-                vel[1, c, at, here] = vv[c, j, at, :]
+                vel_out[0, c, to, here] = uu[c, j, at, :]
+                vel_out[1, c, to, here] = vv[c, j, at, :]
                 p, m = sp_p[c, j, at, :], sp_m[c, j, at, :]
-                st[0, c, at, here] = 0.5 * (p + m) - STRENGTH * h[c, at, here]
-                st[1, c, at, here] = 0.5 * (p - m)
-                st[2, c, at, here] = 0.5 * sp_s[c, j, at, :]
+                stress_out[0, c, to, here] = 0.5 * (p + m) - STRENGTH * h[c, at, here]
+                stress_out[1, c, to, here] = 0.5 * (p - m)
+                stress_out[2, c, to, here] = 0.5 * sp_s[c, j, at, :]
             return 0
 
         lax.fori_loop(0, rows // T, out_chunk, 0, unroll=4)
-        outs = [
-            pltpu.make_async_copy(
-                vel.at[:, c, TOP:end, :], vel_out.at[:, c], out_sem.at[2 * phase]
-            ),
-            pltpu.make_async_copy(
-                st.at[:, c, TOP:end, :], stress_out.at[:, c], out_sem.at[2 * phase + 1]
-            ),
-        ]
-        for copy in outs:
-            copy.start()
-        return outs, icols + fcols
 
     def back_copies(phase, c, source, target):
         at = pl.ds(pl.multiple_of(TOP + source * rows, T), rows)
-        parts = (
-            (sp.at[c, :, 0:rows, :], forcing.at[:, at, :]),
-            (sp.at[c, :, rows : rows + T, :], extra.at[source]),
-        )
+        parts = ((sp.at[c], forcing.at[0:own, at, :]), (trim_s.at[c], trim_r.at[source]))
         return [
             pltpu.make_async_remote_copy(
                 src_ref=src,
                 dst_ref=dst,
-                send_sem=back_send.at[2 * phase + i],
-                recv_sem=back_recv.at[source, i],
+                send_sem=back_send.at[phase],
+                recv_sem=back_recv.at[source],
                 device_id=(target, ti),
                 device_id_type=MESH,
             )
-            for i, (src, dst) in enumerate(parts)
+            for src, dst in parts
         ]
 
     def edge_copies():
         top, bottom = groups - 1, 0
         parts = (
-            (top, 1, sp.at[0, :, rows - T : rows, :], forcing.at[:, TOP - T : TOP, :]),
-            (top, 1, sp.at[0, :, rows : rows + T, :], extra.at[0]),
-            (bottom, groups - 2, sp.at[1, :, 0:T, :], forcing.at[:, oend : oend + T, :]),
+            (0, top, 1, sp.at[0, :, rows - T : rows, :], forcing.at[0:own, TOP - T : TOP, :]),
+            (0, top, 1, trim_s.at[0], trim_r.at[0]),
+            (1, bottom, groups - 2, sp.at[1, :, 0:T, :], forcing.at[0:own, oend : oend + T, :]),
+            (1, bottom, groups - 2, trim_s.at[1], trim_r.at[0]),
         )
         return [
             (
@@ -716,44 +755,86 @@
                 pltpu.make_async_remote_copy(
                     src_ref=src,
                     dst_ref=dst,
-                    send_sem=edge_send.at[i],
-                    recv_sem=edge_recv.at[i],
+                    send_sem=edge_send,
+                    recv_sem=edge_recv,
                     device_id=(target, ti),
                     device_id_type=MESH,
                 ),
             )
-            for i, (source, target, src, dst) in enumerate(parts)
+            for way, source, target, src, dst in parts
         ]
 
-    outs_a, cols_a = ice_cap(0)
-    outs_b, cols_b = ice_cap(1)
-
-    receive_all(orow, gi, groups)
+    back_rows = own * rows + 2 * T
+    edge_rows = own * T + 2 * T
+
+    receive_rows(0, 8 * T)
+    icols_a = pack(0)
+    receive_rows(2, 3 * T)
     ocols = pack_ocean()
+    flow_wait(0, 0)
+    fcols_a = pack_flow(0)
+    receive_all(icols_a, ti, tiles)
+    prep(0)
     receive_all(ocols, ti, tiles)
     prepare_ocean()
+    receive_rows(1, 8 * T)
+    icols_b = pack(1)
+    flow_wait(0, 1)
+    receive_all(fcols_a, ti, tiles)
+    add_flow(0)
+    subcycles(0, 0, NSUB // 2)
+    flow_wait(1, 0)
+    fcols_b = pack_flow(1)
+    subcycles(0, NSUB // 2, NSUB)
+    drag(0)
+    output(0)
+    receive_all(icols_b, ti, tiles)
+    prep(1)
+    flow_wait(1, 1)
+    receive_all(fcols_b, ti, tiles)
+    add_flow(1)
+    subcycles(1, 0, NSUB)
+    drag(1)
+    output(1)
+
+    def rim_of(source, k):
+        lanes_each = L // (2 * (rows // T))
+        turn = (lanes_each + 2 * lanes_each * k) % L
+        value = pltpu.roll(trim_r[source, 0], (L - turn) % L, 1)
+        return jnp.where((lane < lanes_each) | (lane >= L - lanes_each), value, 0.0)
 
     def carry_over(row, source):
         for j in range(span):
             at = (j, slice(row, row + 1), slice(None))
-            forcing[at] = forcing[at] - extra[source, j, T - 1 : T, :]
+            forcing[at] = forcing[at] - trim_r[source, 1, j : j + 1, :]
 
     for cap, home in enumerate(homes):
 
         @pl.when(gi == home)
         def _():
-            for source in range(groups):
-                if source != home:
-                    phase = (source + cap) % 2
-                    for copy in back_copies(phase, cap, source, source):
-                        copy.wait_recv()
+            early = [k for k in range(groups) if k != home and (k + cap) % 2 == 0]
+            late = [k for k in range(groups) if k != home and (k + cap) % 2 == 1]
+            for some in ([home] + early, late):
+                for source in some:
+                    if source != home:
+                        take(w0.at[0, 0:back_rows, :], back_recv.at[source])
+                for source in some:
+                    for k in range(rows // T):
+                        row = TOP + source * rows + k * T
+                        forcing[own, row : row + T, :] = rim_of(source, k)
             for source in range(groups):
                 carry_over(TOP + (source + 1) * rows, source)
 
-    for i, (source, target, copy) in enumerate(edge_copies()):
-        pl.when(gi == target)(copy.wait_recv)
-        if i == 1:
-            pl.when(gi == target)(lambda: carry_over(TOP, 0))
+    @pl.when(gi == 1)
+    def _():
+        take(w0.at[0, 0:edge_rows, :], edge_recv)
+        forcing[own, TOP - T : TOP, :] = rim_of(0, rows // T - 1)
+        carry_over(TOP, 0)
+
+    @pl.when(gi == groups - 2)
+    def _():
+        take(w0.at[0, 0:edge_rows, :], edge_recv)
+        forcing[own, oend : oend + T, :] = rim_of(0, 0)
 
     zero = jnp.zeros((T, L), F32)
 
@@ -828,21 +909,12 @@
             pltpu.make_async_remote_copy(
                 src_ref=src,
                 dst_ref=dst.at[d],
-                send_sem=send.at[d],
-                recv_sem=recv.at[d],
+                send_sem=send,
+                recv_sem=recv,
                 device_id=device(lax.rem(index + d, count)),
                 device_id_type=MESH,
             ).start()
-        for d in range(1, count):
-            copy = pltpu.make_async_remote_copy(
-                src_ref=src,
-                dst_ref=dst.at[d],
-                send_sem=send.at[d],
-                recv_sem=recv.at[d],
-                device_id=device(lax.rem(index + d, count)),
-                device_id_type=MESH,
-            )
-            copy.wait()
+        take(dst.at[1:count], recv)
         for d in range(1, count):
             value = value + dst[d]
         return value
@@ -881,47 +953,45 @@
     def final_chunk(k, _):
         at = pl.ds(pl.multiple_of(TOP + k * T, T), T)
         for j in range(own):
-            xn[at, pl.ds(j * L, L)] = x[j, at, :] + (
+            ssh_out[chunk0(k), pl.ds(j * L, L)] = x[j, at, :] + (
                 c0 * v0[j, at, :] + (c1 * v1[j, at, :] + c2 * v2[j, at, :])
             )
         return 0
 
     lax.fori_loop(0, orows // T, final_chunk, 0, unroll=4)
-    last = pltpu.make_async_copy(xn.at[TOP:oend, :], ssh_out, out_sem.at[4])
-    last.start()
-
-    for way, copy in irow[0] + irow[1] + orow:
-        pl.when(edge(way, gi, groups)[0])(copy.wait_send)
-    for way, copy in ocols + cols_a + cols_b:
-        pl.when(edge(way, ti, tiles)[0])(copy.wait_send)
+    for way in range(2):
+        pl.when(edge(way, gi, groups)[0])(
+            lambda: take(gn.at[0 : 19 * T, :], row_send.at[way])
+        )
+        sent = 2 * (rows + 2 * T) + (orows + 2 * T) // 2
+        pl.when(edge(way, ti, tiles)[0])(lambda: take(w0.at[0:2, 0:sent, :], col_send.at[way]))
     for cap, home in enumerate(homes):
 
         @pl.when(gi == home)
         def _():
-            for target in range(groups):
-                if target != home:
-                    for piece in range(3):
-                        flow_copy(cap, target, piece).wait_send()
+            spans = [flow_span(k) for k in range(groups) if k != home]
+            take(cur_in.at[:, 0 : sum(hi - lo for lo, hi, _ in spans), :], flow_send)
 
     for phase in range(2):
-        c = lax.rem(gi + phase, 2)
-
-        @pl.when(gi != c * (groups - 1))
-        def _():
-            for copy in back_copies(phase, c, gi, c * (groups - 1)):
-                copy.wait_send()
-
-    for source, target, copy in edge_copies():
-        pl.when(gi == source)(copy.wait_send)
-    for copy in outs_a + outs_b:
+        pl.when(gi != lax.rem(gi + phase, 2) * (groups - 1))(
+            lambda: take(w0.at[0, 0:back_rows, :], back_send.at[phase])
+        )
+    pl.when((gi == 0) | (gi == groups - 1))(lambda: take(w0.at[0, 0:edge_rows, :], edge_send))
+    take(red_r.at[1:tiles], red_send)
+    take(red2_r.at[1:groups], red2_send)
+
+
+def deliver(*refs):
+    sems = refs[-1]
+    half = len(refs) // 2
+    copies = [
+        pltpu.make_async_copy(src, dst, sems.at[k])
+        for k, (src, dst) in enumerate(zip(refs[:half], refs[half:-1]))
+    ]
+    for copy in copies:
+        copy.start()
+    for copy in copies:
         copy.wait()
-    last.wait()
-
-
-def deliver(*refs):
-    half = len(refs) // 2
-    for src, dst in zip(refs[:half], refs[half:]):
-        dst[...] = src[...]
 
 
 def step(groups, tiles, *args):
@@ -931,7 +1001,6 @@
     irows = rows + 2 * TOP
     erows = orows + 2 * TOP
     span = cols // L + 1
-    any_spec = pl.BlockSpec(memory_space=pl.ANY)
     hbm = pl.BlockSpec(memory_space=pltpu.HBM)
     vmem = pl.BlockSpec(memory_space=pltpu.VMEM)
     dma = pltpu.SemaphoreType.DMA
@@ -941,13 +1010,15 @@
     results = pl.pallas_call(
         functools.partial(kernel, groups, tiles),
         out_shape=(
-            jax.ShapeDtypeStruct(base_rhs.shape, F32),
-            jax.ShapeDtypeStruct(ice_vel.shape, F32),
-            jax.ShapeDtypeStruct(ice_stress.shape, F32),
+            pltpu.VMEM(base_rhs.shape, F32),
+            pltpu.VMEM(ice_vel.shape, F32),
+            pltpu.VMEM(ice_stress.shape, F32),
         ),
-        in_specs=[hbm] * 4 + [vmem, hbm, vmem] + [hbm] * 3,
-        out_specs=(any_spec,) * 3,
+        in_specs=[hbm] * 10,
+        out_specs=(vmem,) * 3,
         scratch_shapes=[
+            pltpu.VMEM(args[4].shape, jnp.int32),
+            pltpu.VMEM(args[6].shape, jnp.int32),
             pltpu.VMEM((2, 2, irows, cols), F32),
             pltpu.VMEM((3, 2, irows, cols), F32),
             pltpu.VMEM((2, 2, irows, cols), F32),
@@ -972,38 +1043,40 @@
             pltpu.VMEM((2, 2, rows + 2 * T, L), F32),
             pltpu.VMEM((2, orows + 2 * T, L), F32),
             pltpu.VMEM((2, orows + 2 * T, L), F32),
-            pltpu.VMEM((2, span, rows + T, L), F32),
-            pltpu.VMEM((groups, span, T, L), F32),
+            pltpu.VMEM((2, span - 1, rows, L), F32),
+            pltpu.VMEM((2, 2, T, L), F32),
+            pltpu.VMEM((groups, 2, T, L), F32),
             pltpu.VMEM((T, L), F32),
             pltpu.VMEM((tiles, T, L), F32),
             pltpu.VMEM((T, L), F32),
             pltpu.VMEM((groups, T, L), F32),
-            dma((7,)),
-            dma((3 * groups,)),
+            dma((9,)),
+            dma,
+            dma((4,)),
+            dma((2,)),
             dma((6,)),
-            dma((22,)),
-            dma((22,)),
+            dma((2,)),
             dma((10,)),
-            dma((10,)),
-            dma((4,)),
-            dma((groups, 2)),
-            dma((3,)),
-            dma((3,)),
-            dma((tiles,)),
-            dma((tiles,)),
+            dma((2,)),
             dma((groups,)),
-            dma((groups,)),
-            dma((5,)),
+            dma,
+            dma,
+            dma,
+            dma,
+            dma,
+            dma,
         ],
         compiler_params=pltpu.CompilerParams(
-            collective_id=0, has_side_effects=True, vmem_limit_bytes=67_043_328
+            collective_id=0, has_side_effects=True, vmem_limit_bytes=48 * 2**20
         ),
-    )(*args)
+    )(*(pltpu.with_memory_space_constraint(a, pltpu.HBM) for a in args))
     return pl.pallas_call(
         deliver,
         out_shape=tuple(jax.ShapeDtypeStruct(r.shape, F32) for r in results),
         in_specs=[vmem] * 3,
-        out_specs=(vmem,) * 3,
+        out_specs=(hbm,) * 3,
+        scratch_shapes=[dma((3,))],
+        compiler_params=pltpu.CompilerParams(vmem_limit_bytes=4 * 2**20),
     )(*results)
 
 

time: 53.2 us -> 48 us (0.902)
  Pallas kernels: 52.3 us -> 47.1 us
    pallas_call x1, Pallas kernels: 49.6 us -> 45.8 us  [step(): pl.pallas_call(functools.partial(kernel, groups, tiles), out_shape=(pltpu...]
    pallas_call x1, Pallas kernels: 2.71 us -> 1.25 us  [step(): pl.pallas_call(deliver, out_shape=tuple((jax.ShapeDtypeStruct(r.shape, F3...]
where the time goes in v3:
time: 48 us; the launch traced here: 47.7 us
  Pallas kernels  47.1 us (98%)
  between operations  0.64 us (1%)
    pallas_call x1, Pallas kernels, step(): pl.pallas_call(functools.partial(kernel, groups, tiles), out_shape=(pltpu...  45.8 us
    pallas_call x1, Pallas kernels, step(): pl.pallas_call(deliver, out_shape=tuple((jax.ShapeDtypeStruct(r.shape, F3...  1.25 us

profile of v3, /device:TPU:0, one launch (start us, length us, event | category | flops | bytes accessed | tf_op | source)
XLA Modules:
  0.0 47.7 jit_solution(1587733184218314868)
XLA Ops:
  0.6 45.8 %shard_map.121 = (f32[256,512]{1,0:T(8,128)S(1)}, f32[2,2,64,512]{3,2,1,0:T(8,128)S(1)}, f32[3,2,64,512]{3,2,1,0:T(8,128)S(1)}) custom-call(f32[256,512]{1,0:T(8,128)} %base_in.1, f32[256,512]{1,0:T(8,128)} %depth_in.1, f32[256,512]{1,0:T(8,128)} %ssh_in.1, f32[2,256,512]{2,1,0:T(8,128)} %cur_in.1, s32[32,64]{1,0:T(8,128)} %land_in.1, ...), custom_call_target="tpu_custom_call" | custom-call | tf_op jit(solution)/shard_map/pallas_call | solution.py:1010
  46.5 1.3 %shard_map.122 = (f32[256,512]{1,0:T(8,128)}, f32[2,2,64,512]{3,2,1,0:T(8,128)}, f32[3,2,64,512]{3,2,1,0:T(8,128)}) custom-call(f32[256,512]{1,0:T(8,128)S(1)} %get-tuple-element.6.refs_0_, f32[2,2,64,512]{3,2,1,0:T(8,128)S(1)} %get-tuple-element.7.refs_1_, f32[3,2,64,512]{3,2,1,0:T(8,128)S(1)} %get-tuple-element.8.refs_2_), custom_call_target="tpu_custom_call" | custom-call | tf_op jit(solution)/shard_map/pallas_call | solution.py:1073

commit v4 on v3

--- a/solution.py
+++ b/solution.py
@@ -127,8 +127,6 @@
     trim_r,
     red_s,
     red_r,
-    red2_s,
-    red2_r,
     load_sem,
     flow_send,
     flow_recv,
@@ -142,8 +140,7 @@
     edge_recv,
     red_send,
     red_recv,
-    red2_send,
-    red2_recv,
+    ready,
 ):
     gi = lax.axis_index("grp")
     ti = lax.axis_index("tile")
@@ -216,9 +213,6 @@
     for ref in (g, gx, w0, w1, w2):
         clear(ref, (0, T), (oend + T, oend + 2 * T))
 
-    load_land.wait()
-    load_ice.wait()
-
     def blocks(ref, out, count):
         width = ref.shape[-1]
         row = lax.broadcasted_iota(jnp.int32, (width, cols), 0)
@@ -226,13 +220,11 @@
         values = ref[...].reshape((count, width)).astype(F32)
         out[...] = jnp.dot(values, spread, preferred_element_type=F32)
 
-    blocks(land_ref, wet, land_ref.shape[0])
-    for c in range(2):
-        row = lax.broadcasted_iota(jnp.int32, (cols // BS, cols), 0)
-        spread = (row == lax.shift_right_logical(lanes(cols // BS, cols), 3)).astype(F32)
-        cover[c] = jnp.dot(ice_ref[c].astype(F32), spread, preferred_element_type=F32)
-
     pl.semaphore_wait(barrier, groups + tiles - 2)
+    for d in range(1, tiles):
+        pl.semaphore_signal(
+            ready, inc=1, device_id=(gi, lax.rem(ti + d, tiles)), device_id_type=MESH
+        )
 
     homes = (0, groups - 1)
     pieces = ((0, L), (cols - L, cols), (L, cols - L))
@@ -294,19 +286,22 @@
                         (rows, end),
                     )
                 )
-        for way in range(2):
-            out.append(
-                row_copy(
-                    stage,
-                    way,
-                    lambda at: h.at[c, at, :],
-                    lambda at: h.at[c, at, :],
-                    TOP,
-                    TOP,
-                    (rows, end),
-                )
+        return out
+
+    def thick_rows(stage):
+        c = lax.rem(gi + 1 + stage, 2)
+        return [
+            row_copy(
+                stage,
+                way,
+                lambda at: h.at[c, at, :],
+                lambda at: h.at[c, at, :],
+                TOP,
+                TOP,
+                (rows, end),
             )
-        return out
+            for way in range(2)
+        ]
 
     def ocean_rows():
         return [
@@ -349,6 +344,17 @@
             for piece in range(3):
                 flow_copy(cap, home, piece).start()
 
+    load_vel.wait()
+    load_st.wait()
+    load_wind.wait()
+    start_all(ice_rows(0), gi, groups)
+    load_land.wait()
+    load_ice.wait()
+    blocks(land_ref, wet, land_ref.shape[0])
+    for c in range(2):
+        row = lax.broadcasted_iota(jnp.int32, (cols // BS, cols), 0)
+        spread = (row == lax.shift_right_logical(lanes(cols // BS, cols), 3)).astype(F32)
+        cover[c] = jnp.dot(ice_ref[c].astype(F32), spread, preferred_element_type=F32)
     load_thick.wait()
 
     def cover_chunk(k, _):
@@ -358,10 +364,7 @@
         return 0
 
     lax.fori_loop(0, rows // T, cover_chunk, 0, unroll=4)
-    load_vel.wait()
-    load_st.wait()
-    load_wind.wait()
-    start_all(ice_rows(0), gi, groups)
+    start_all(thick_rows(0), gi, groups)
     load_depth.wait()
 
     def wet_chunk(k, _):
@@ -386,6 +389,7 @@
 
     send_flow(lambda order: order[1:])
     start_all(ice_rows(1), gi, groups)
+    start_all(thick_rows(1), gi, groups)
     send_flow(lambda order: order[:1])
 
     lane = lanes(T, L)
@@ -857,7 +861,7 @@
 
     first_chunk(0)
     first_chunk(ochunks - 1)
-    m0 = lax.fori_loop(1, ochunks - 1, lambda k, s: s + first_chunk(k), zero, unroll=4)
+    m0 = lax.fori_loop(1, ochunks - 1, lambda k, s: s + first_chunk(k), zero, unroll=8)
 
     def power(w_from, v_to, w_to):
         def body(k, turns):
@@ -878,53 +882,53 @@
         body(ochunks - 1, turned(w_from, ochunks - 1))
 
         def step(k, carry):
-            turns, s0, s1 = carry
-            ahead = turned(w_from, k + 1)
+            turns, after, s0, s1 = carry
+            ahead = turned(w_from, k + 2)
             a, b = body(k, turns)
-            return ahead, s0 + a, s1 + b
-
-        carry = (turned(w_from, 1), zero, zero)
-        _, s0, s1 = lax.fori_loop(1, ochunks - 1, step, carry, unroll=8)
+            return after, ahead, s0 + a, s1 + b
+
+        carry = (turned(w_from, 1), turned(w_from, 2), zero, zero)
+        _, _, s0, s1 = lax.fori_loop(1, ochunks - 1, step, carry, unroll=ochunks - 2)
         return s0, s1
 
     m1, m2 = power(w0, v1, w1)
     m3, m4 = power(w1, v2, w2)
 
     def last_step(k, carry):
-        turns, s = carry
-        ahead = turned(w2, k + 1)
+        turns, after, s = carry
+        ahead = turned(w2, k + 2)
         near = around(w2, k, *turns)
-        return ahead, s + fold([w2[j, chunk(k), :] for j in range(own)], near)
-
-    _, m5 = lax.fori_loop(1, ochunks - 1, last_step, (turned(w2, 1), zero), unroll=8)
+        return after, ahead, s + fold([w2[j, chunk(k), :] for j in range(own)], near)
+
+    carry = (turned(w2, 1), turned(w2, 2), zero)
+    _, _, m5 = lax.fori_loop(1, ochunks - 1, last_step, carry, unroll=ochunks - 2)
 
     row = lax.broadcasted_iota(jnp.int32, (T, L), 0)
     moments = zero
     for k, m in enumerate((m0, m1, m2, m3, m4, m5)):
         moments = jnp.where(row == k, jnp.sum(m, axis=0, keepdims=True), moments)
 
-    def all_reduce(value, src, dst, send, recv, index, count, device):
-        src[...] = value
-        for d in range(1, count):
-            pltpu.make_async_remote_copy(
-                src_ref=src,
-                dst_ref=dst.at[d],
-                send_sem=send,
-                recv_sem=recv,
-                device_id=device(lax.rem(index + d, count)),
-                device_id_type=MESH,
-            ).start()
-        take(dst.at[1:count], recv)
-        for d in range(1, count):
-            value = value + dst[d]
-        return value
-
-    moments = all_reduce(
-        moments, red_s, red_r, red_send, red_recv, ti, tiles, lambda k: (gi, k)
-    )
-    moments = all_reduce(
-        moments, red2_s, red2_r, red2_send, red2_recv, gi, groups, lambda k: (k, ti)
-    )
+    lane_sums = jnp.sum(moments, axis=1, keepdims=True)
+    diagonal = lanes(T, L) == row
+    red_s[...] = jnp.sum(jnp.where(diagonal, lane_sums, 0.0), axis=0, keepdims=True)
+
+    pl.semaphore_wait(ready, tiles - 1)
+    count = groups * tiles
+    for d in range(1, count):
+        other = lax.rem(gi * tiles + ti + d, count)
+        pltpu.make_async_remote_copy(
+            src_ref=red_s,
+            dst_ref=red_r.at[d],
+            send_sem=red_send,
+            recv_sem=red_recv,
+            device_id=(lax.div(other, tiles), lax.rem(other, tiles)),
+            device_id_type=MESH,
+        ).start()
+    take(red_r.at[1:count], red_recv)
+    parts = [red_s[...]] + [red_r[d] for d in range(1, count)]
+    while len(parts) > 1:
+        parts = [sum(parts[i : i + 2]) for i in range(0, len(parts), 2)]
+    moments = jnp.where(diagonal, parts[0], 0.0)
     total = jnp.sum(moments, axis=1, keepdims=True)
     nu = [total[k : k + 1, :] for k in range(6)]
     a = [nu[k] - nu[k + 1] for k in range(5)]
@@ -958,7 +962,7 @@
             )
         return 0
 
-    lax.fori_loop(0, orows // T, final_chunk, 0, unroll=4)
+    lax.fori_loop(0, orows // T, final_chunk, 0, unroll=16)
     for way in range(2):
         pl.when(edge(way, gi, groups)[0])(
             lambda: take(gn.at[0 : 19 * T, :], row_send.at[way])
@@ -977,8 +981,7 @@
             lambda: take(w0.at[0, 0:back_rows, :], back_send.at[phase])
         )
     pl.when((gi == 0) | (gi == groups - 1))(lambda: take(w0.at[0, 0:edge_rows, :], edge_send))
-    take(red_r.at[1:tiles], red_send)
-    take(red2_r.at[1:groups], red2_send)
+    take(red_r.at[1:count], red_send)
 
 
 def deliver(*refs):
@@ -1046,10 +1049,8 @@
             pltpu.VMEM((2, span - 1, rows, L), F32),
             pltpu.VMEM((2, 2, T, L), F32),
             pltpu.VMEM((groups, 2, T, L), F32),
-            pltpu.VMEM((T, L), F32),
-            pltpu.VMEM((tiles, T, L), F32),
-            pltpu.VMEM((T, L), F32),
-            pltpu.VMEM((groups, T, L), F32),
+            pltpu.VMEM((1, L), F32),
+            pltpu.VMEM((groups * tiles, 1, L), F32),
             dma((9,)),
             dma,
             dma((4,)),
@@ -1063,8 +1064,7 @@
             dma,
             dma,
             dma,
-            dma,
-            dma,
+            pltpu.SemaphoreType.REGULAR,
         ],
         compiler_params=pltpu.CompilerParams(
             collective_id=0, has_side_effects=True, vmem_limit_bytes=48 * 2**20

time: 48 us -> 44.6 us (0.929)
  Pallas kernels: 47.1 us -> 43.8 us
    pallas_call x1, Pallas kernels: 45.8 us -> 42.6 us  [step(): pl.pallas_call(functools.partial(kernel, groups, tiles), out_shape=(pltpu...]
where the time goes in v4:
time: 44.6 us; the launch traced here: 44.5 us
  Pallas kernels  43.8 us (98%)
  between operations  0.64 us (1%)
    pallas_call x1, Pallas kernels, step(): pl.pallas_call(functools.partial(kernel, groups, tiles), out_shape=(pltpu...  42.6 us
    pallas_call x1, Pallas kernels, step(): pl.pallas_call(deliver, out_shape=tuple((jax.ShapeDtypeStruct(r.shape, F3...  1.25 us

profile of v4, /device:TPU:0, one launch (start us, length us, event | category | flops | bytes accessed | tf_op | source)
XLA Modules:
  0.0 44.5 jit_solution(179721434453815681)
XLA Ops:
  0.6 42.6 %shard_map.121 = (f32[256,512]{1,0:T(8,128)S(1)}, f32[2,2,64,512]{3,2,1,0:T(8,128)S(1)}, f32[3,2,64,512]{3,2,1,0:T(8,128)S(1)}) custom-call(f32[256,512]{1,0:T(8,128)} %base_in.1, f32[256,512]{1,0:T(8,128)} %depth_in.1, f32[256,512]{1,0:T(8,128)} %ssh_in.1, f32[2,256,512]{2,1,0:T(8,128)} %cur_in.1, s32[32,64]{1,0:T(8,128)} %land_in.1, ...), custom_call_target="tpu_custom_call" | custom-call | tf_op jit(solution)/shard_map/pallas_call | solution.py:1013
  43.2 1.3 %shard_map.122 = (f32[256,512]{1,0:T(8,128)}, f32[2,2,64,512]{3,2,1,0:T(8,128)}, f32[3,2,64,512]{3,2,1,0:T(8,128)}) custom-call(f32[256,512]{1,0:T(8,128)S(1)} %get-tuple-element.6.refs_0_, f32[2,2,64,512]{3,2,1,0:T(8,128)S(1)} %get-tuple-element.7.refs_1_, f32[3,2,64,512]{3,2,1,0:T(8,128)S(1)} %get-tuple-element.8.refs_2_), custom_call_target="tpu_custom_call" | custom-call | tf_op jit(solution)/shard_map/pallas_call | solution.py:1073

commit v5 on v4

--- a/solution.py
+++ b/solution.py
@@ -152,6 +152,8 @@
     span = own + 1
     ichunks = rows // T + 2
     ochunks = orows // T + 2
+    split = rows - 2 * T
+    above_split, below_split = (0, split // T + 2), (split // T, ichunks)
 
     barrier = pltpu.get_barrier_semaphore()
     for d in range(1, groups):
@@ -234,22 +236,34 @@
         hi = min(rows * groups, rows * target + rows + T)
         return lo, hi, TOP + lo - rows * target
 
-    def flow_copy(cap, target, piece):
+    def flow_parts(cap, target):
         lo, hi, start = flow_span(target)
-        first, last = pieces[piece]
-        src = cur_in.at[:, lo:hi, first:last]
-        dst = flow.at[:, cap, start : start + hi - lo, first:last]
-        recv = flow_recv.at[2 * cap + piece // 2]
-        if target == homes[cap]:
-            return pltpu.make_async_copy(src, dst, recv)
-        return pltpu.make_async_remote_copy(
-            src_ref=src,
-            dst_ref=dst,
-            send_sem=flow_send,
-            recv_sem=recv,
-            device_id=(target, ti),
-            device_id_type=MESH,
-        )
+        if (cap + target) % 2 == 0:
+            return ((lo, hi, start),)
+        middle = TOP + split + T
+        return ((lo, lo + middle - start, start), (lo + middle - start, hi, middle))
+
+    def flow_copies(cap, target):
+        out = []
+        for part, (lo, hi, start) in enumerate(flow_parts(cap, target)):
+            for piece, (first, last) in enumerate(pieces):
+                src = cur_in.at[:, lo:hi, first:last]
+                dst = flow.at[:, cap, start : start + hi - lo, first:last]
+                recv = flow_recv.at[4 * cap + 2 * part + piece // 2]
+                if target == homes[cap]:
+                    out.append(pltpu.make_async_copy(src, dst, recv))
+                else:
+                    out.append(
+                        pltpu.make_async_remote_copy(
+                            src_ref=src,
+                            dst_ref=dst,
+                            send_sem=flow_send,
+                            recv_sem=recv,
+                            device_id=(target, ti),
+                            device_id_type=MESH,
+                        )
+                    )
+        return out
 
     def take(ref, sem):
         pltpu.make_async_copy(ref, ref, sem).wait()
@@ -341,8 +355,8 @@
 
         @pl.when(gi == home)
         def _():
-            for piece in range(3):
-                flow_copy(cap, home, piece).start()
+            for copy in flow_copies(cap, home):
+                copy.start()
 
     load_vel.wait()
     load_st.wait()
@@ -384,8 +398,8 @@
             def _():
                 order = sorted((k for k in range(groups) if k != home), key=lambda k: abs(k - home))
                 for target in which(order):
-                    for piece in range(3):
-                        flow_copy(cap, target, piece).start()
+                    for copy in flow_copies(cap, target):
+                        copy.start()
 
     send_flow(lambda order: order[1:])
     start_all(ice_rows(1), gi, groups)
@@ -489,11 +503,12 @@
                 inverse = jnp.where(thick > 0.0, 1.0 / (mass + STEP * DRAG), 0.0)
                 q = STEP * inverse
                 half = 0.5 * q
-                uu[c, j, at, :] = u
-                vv[c, j, at, :] = v
-                sp_p[c, j, at, :] = (s0 + s1) + STRENGTH * thick
-                sp_m[c, j, at, :] = (s0 - s1) + STRENGTH * thick
-                sp_s[c, j, at, :] = s2 + s2
+                for slot in (c,) if phase == 0 else (c, 2):
+                    uu[slot, j, at, :] = u
+                    vv[slot, j, at, :] = v
+                    sp_p[slot, j, at, :] = (s0 + s1) + STRENGTH * thick
+                    sp_m[slot, j, at, :] = (s0 - s1) + STRENGTH * thick
+                    sp_s[slot, j, at, :] = s2 + s2
                 kk[c, j, at, :] = RATE * thick
                 pp[c, j, at, :] = mass * inverse
                 qq[c, j, at, :] = half
@@ -548,19 +563,25 @@
         lax.fori_loop(0, ochunks, ocean_chunk, 0, unroll=steps)
         lax.fori_loop(0, ochunks, pre_chunk, (turned(g, 0), turned(gx, 0)), unroll=steps)
 
-    def flow_wait(phase, part):
+    def flow_wait(phase, part, piece):
         for target in range(groups):
 
             @pl.when(gi == target)
             def _():
                 cap = (target + phase) % 2
-                lo, hi, start = flow_span(target)
-                width = 2 * L if part == 0 else cols - 2 * L
+                lo, hi, start = flow_parts(cap, target)[part]
+                width = 2 * L if piece == 0 else cols - 2 * L
                 ref = flow.at[:, cap, start : start + hi - lo, 0:width]
-                take(ref, flow_recv.at[2 * cap + part])
-
-    def pack_flow(phase):
+                take(ref, flow_recv.at[4 * cap + 2 * part + piece])
+
+    def flow_chunks(phase, part):
+        if phase == 0:
+            return 0, ichunks
+        return (0, above_split[1]) if part == 0 else (above_split[1], ichunks)
+
+    def pack_flow(phase, part):
         c = lax.rem(gi + phase, 2)
+        first, last = flow_chunks(phase, part)
 
         def fpack_chunk(k, _):
             after, before = packed(ends((flow.at[0, c], flow.at[1, c]), chunk(k)))
@@ -568,15 +589,19 @@
             fpack_s[1, c, chunk0(k), :] = before
             return 0
 
-        lax.fori_loop(0, ichunks, fpack_chunk, 0, unroll=ichunks)
+        lax.fori_loop(first, last, fpack_chunk, 0, unroll=last - first)
+        at = slice(first * T, last * T)
         fcols = col_copies(
-            lambda way: fpack_s.at[way, c], lambda way: fpack_r.at[way, c], 4 * phase + 2
+            lambda way: fpack_s.at[way, c, at, :],
+            lambda way: fpack_r.at[way, c, at, :],
+            (2 if phase == 0 else 6) if part == 0 else 10,
         )
         start_all(fcols, ti, tiles)
         return fcols
 
-    def add_flow(phase):
+    def add_flow(phase, part):
         c = lax.rem(gi + phase, 2)
+        first, last = flow_chunks(phase, part)
 
         def flow_chunk(k, _):
             at = chunk(k)
@@ -591,10 +616,12 @@
                     )
             return 0
 
-        lax.fori_loop(0, ichunks, flow_chunk, 0, unroll=ichunks)
-
-    def subcycles(phase, first, last):
+        lax.fori_loop(first, last, flow_chunk, 0, unroll=last - first)
+
+    def subcycles(phase, part, first, last):
         c = lax.rem(gi + phase, 2)
+        slot = 2 if part == 1 else c
+        low, high = (0, ichunks) if phase == 0 else (above_split, below_split)[part]
 
         def subcycle(n, _):
             ahead, behind = 2, 2
@@ -602,26 +629,26 @@
 
             def look(k):
                 at = slice(T + T * k, TOP + T * k)
-                turned_u[k] = turn_right([uu[c, j, at, :] for j in range(span)])
-                turned_v[k] = turn_right([vv[c, j, at, :] for j in range(span)])
+                turned_u[k] = turn_right([uu[slot, j, at, :] for j in range(span)])
+                turned_v[k] = turn_right([vv[slot, j, at, :] for j in range(span)])
 
             def stress(k):
                 at, down = slice(T + T * k, TOP + T * k), slice(T + T * k + 1, TOP + T * k + 1)
                 beside_u, beside_v = join_right(turned_u.pop(k)), join_right(turned_v.pop(k))
                 ms, ss = [], []
                 for j in range(span):
-                    u, v = uu[c, j, at, :], vv[c, j, at, :]
-                    du = uu[c, j, down, :] - u
+                    u, v = uu[slot, j, at, :], vv[slot, j, at, :]
+                    du = uu[slot, j, down, :] - u
                     dv = beside_v[j] - v
-                    shear = (beside_u[j] - u) + (vv[c, j, down, :] - v)
+                    shear = (beside_u[j] - u) + (vv[slot, j, down, :] - v)
                     rate = kk[c, j, at, :] * lax.rsqrt(
                         (du * du + dv * dv) + (0.5 * (shear * shear) + 0.5)
                     )
-                    sp_p[c, j, at, :] = sp_p[c, j, at, :] * KEEP + rate * du
-                    m = sp_m[c, j, at, :] * KEEP + rate * dv
-                    s = sp_s[c, j, at, :] * KEEP + rate * shear
-                    sp_m[c, j, at, :] = m
-                    sp_s[c, j, at, :] = s
+                    sp_p[slot, j, at, :] = sp_p[slot, j, at, :] * KEEP + rate * du
+                    m = sp_m[slot, j, at, :] * KEEP + rate * dv
+                    s = sp_s[slot, j, at, :] * KEEP + rate * shear
+                    sp_m[slot, j, at, :] = m
+                    sp_s[slot, j, at, :] = s
                     ms.append(m)
                     ss.append(s)
                 turned_m[k], turned_s[k] = turn_left(ms), turn_left(ss)
@@ -630,74 +657,78 @@
                 at, up = slice(T + T * k, TOP + T * k), slice(T + T * k - 1, TOP + T * k - 1)
                 beside_m, beside_s = join_left(turned_m.pop(k)), join_left(turned_s.pop(k))
                 for j in range(span):
-                    s = sp_s[c, j, at, :]
-                    fx = (sp_p[c, j, at, :] - sp_p[c, j, up, :]) + (s - beside_s[j])
-                    fy = (sp_m[c, j, at, :] - beside_m[j]) + (s - sp_s[c, j, up, :])
+                    s = sp_s[slot, j, at, :]
+                    fx = (sp_p[slot, j, at, :] - sp_p[slot, j, up, :]) + (s - beside_s[j])
+                    fy = (sp_m[slot, j, at, :] - beside_m[j]) + (s - sp_s[slot, j, up, :])
                     p, q = pp[c, j, at, :], qq[c, j, at, :]
-                    uu[c, j, at, :] = p * uu[c, j, at, :] + (q * fx + ww[0, c, j, at, :])
-                    vv[c, j, at, :] = p * vv[c, j, at, :] + (q * fy + ww[1, c, j, at, :])
-
-            for k in range(-ahead, ichunks + behind):
-                if k + ahead < ichunks:
+                    uu[slot, j, at, :] = p * uu[slot, j, at, :] + (q * fx + ww[0, c, j, at, :])
+                    vv[slot, j, at, :] = p * vv[slot, j, at, :] + (q * fy + ww[1, c, j, at, :])
+
+            for k in range(low - ahead, high + behind):
+                if k + ahead < high:
                     look(k + ahead)
-                if 0 <= k < ichunks:
+                if low <= k < high:
                     stress(k)
-                if 0 <= k - behind < ichunks:
+                if low <= k - behind < high:
                     momentum(k - behind)
             return 0
 
-        lax.fori_loop(first, last, subcycle, 0)
-
-    def drag(phase):
+        lax.fori_loop(first, last, subcycle, 0, unroll=2)
+
+    def owned_rows(phase, part):
+        if phase == 0:
+            return 0, rows
+        return (0, split) if part == 0 else (split, rows)
+
+    def drag(phase, part):
         c = lax.rem(gi + phase, 2)
+        slot = 2 if part == 1 else c
         home = c * (groups - 1)
         edge_lanes = L // (2 * (rows // T))
-
-        def drag_chunk(k, drag_up):
-            at = pl.ds(pl.multiple_of(TOP + k * T, T), T)
-            drags = []
-            for comp, ref in enumerate((uu, vv)):
-                values = [flow[comp, c, at, pl.ds(j * L, L)] for j in range(own)]
-                values.append(flow_edge[comp, c, at, :])
-                drags.append(
-                    [
-                        jnp.where(qq[c, j, at, :] > 0.0, DRAG * (ref[c, j, at, :] - values[j]), 0.0)
-                        for j in range(span)
-                    ]
-                )
-            beside = left(drags[1])
-            for j in range(span):
-                d0 = drags[0][j]
-                d0_up = above(drag_up[j], d0)
-                value = (d0 - d0_up) + (drags[1][j] - beside[j])
-                if j < own:
-                    sp[c, j, chunk0(k), :] = value
-                else:
-                    rim = value
-            return tuple(drags[0]), rim
+        first, last = (row // T for row in owned_rows(phase, part))
+
+        def drag_values(k, comp, slot):
+            at = pl.ds(TOP + k * T, T)
+            values = [flow[comp, c, at, pl.ds(j * L, L)] for j in range(own)]
+            values.append(flow_edge[comp, c, at, :])
+            ref = (uu, vv)[comp]
+            return [
+                jnp.where(qq[c, j, at, :] > 0.0, DRAG * (ref[slot, j, at, :] - values[j]), 0.0)
+                for j in range(span)
+            ]
 
         zero = jnp.zeros((T, L), F32)
-        upper, rims = (zero,) * span, zero
-        for k in range(rows // T):
-            upper, rim = drag_chunk(k, upper)
+        upper, rims = [zero] * span if part == 0 else drag_values(first - 1, 0, c), zero
+        for k in range(first, last):
+            across, along = drag_values(k, 0, slot), drag_values(k, 1, slot)
+            beside = left(along)
+            value = [
+                (across[j] - above(upper[j], across[j])) + (along[j] - beside[j])
+                for j in range(span)
+            ]
+            for j in range(own):
+                sp[c, j, k * T : k * T + T, :] = value[j]
             width = 2 * edge_lanes
             here = (lane >= width * k) & (lane < width * k + width)
-            rims = jnp.where(here, pltpu.roll(rim, (edge_lanes + width * k) % L, 1), rims)
-        trim_s[c, 0] = rims
+            rims = jnp.where(here, pltpu.roll(value[own], (edge_lanes + width * k) % L, 1), rims)
+            upper = across
+        trim_s[slot, 0] = rims
         row = lax.broadcasted_iota(jnp.int32, (T, L), 0)
-        last = zero
+        final = zero
         for j in range(span):
-            last = jnp.where(row == j, upper[j][T - 1 : T, :], last)
-        trim_s[c, 1] = last
+            final = jnp.where(row == j, upper[j][T - 1 : T, :], final)
+        trim_s[slot, 1] = final
 
         @pl.when(gi != home)
         def _():
-            for copy in back_copies(phase, c, gi, home):
+            for copy in back_copies(phase, part, c, gi, home):
                 copy.start()
 
         if phase == 1:
             for source, target, copy in edge_copies():
-                pl.when(gi == source)(copy.start)
+                if (source == 0) == (part == 0):
+                    pl.when(gi == source)(copy.start)
+            return
 
         @pl.when(gi == home)
         def _():
@@ -709,48 +740,59 @@
                     return 0
 
                 lax.fori_loop(0, rows // T, own_chunk, 0, unroll=rows // T)
-            trim_r[gi] = trim_s[c]
-
-    def output(phase):
+            trim_r[gi, 0] = trim_s[c]
+
+    def output(phase, part):
         c = lax.rem(gi + phase, 2)
+        slot = 2 if part == 1 else c
+        first, last = (row // T for row in owned_rows(phase, part))
 
         def out_chunk(k, _):
             at = pl.ds(pl.multiple_of(TOP + k * T, T), T)
             to = chunk0(k)
             for j in range(own):
                 here = pl.ds(j * L, L)
-                vel_out[0, c, to, here] = uu[c, j, at, :]
-                vel_out[1, c, to, here] = vv[c, j, at, :]
-                p, m = sp_p[c, j, at, :], sp_m[c, j, at, :]
+                vel_out[0, c, to, here] = uu[slot, j, at, :]
+                vel_out[1, c, to, here] = vv[slot, j, at, :]
+                p, m = sp_p[slot, j, at, :], sp_m[slot, j, at, :]
                 stress_out[0, c, to, here] = 0.5 * (p + m) - STRENGTH * h[c, at, here]
                 stress_out[1, c, to, here] = 0.5 * (p - m)
-                stress_out[2, c, to, here] = 0.5 * sp_s[c, j, at, :]
+                stress_out[2, c, to, here] = 0.5 * sp_s[slot, j, at, :]
             return 0
 
-        lax.fori_loop(0, rows // T, out_chunk, 0, unroll=4)
-
-    def back_copies(phase, c, source, target):
-        at = pl.ds(pl.multiple_of(TOP + source * rows, T), rows)
-        parts = ((sp.at[c], forcing.at[0:own, at, :]), (trim_s.at[c], trim_r.at[source]))
+        lax.fori_loop(first, last, out_chunk, 0, unroll=2)
+
+    def back_copies(phase, part, c, source, target):
+        first, last = owned_rows(phase, part)
+        slot = 2 if part == 1 else c
+        at = pl.ds(pl.multiple_of(TOP + source * rows + first, T), last - first)
+        parts = (
+            (sp.at[c, :, first:last, :], forcing.at[0:own, at, :]),
+            (trim_s.at[slot], trim_r.at[source, part]),
+        )
         return [
             pltpu.make_async_remote_copy(
                 src_ref=src,
                 dst_ref=dst,
-                send_sem=back_send.at[phase],
-                recv_sem=back_recv.at[source],
+                send_sem=back_send.at[phase + part],
+                recv_sem=back_recv.at[source, part],
                 device_id=(target, ti),
                 device_id_type=MESH,
             )
             for src, dst in parts
         ]
 
+    def back_bytes(phase, part):
+        first, last = owned_rows(phase, part)
+        return w0.at[0, 0 : own * (last - first) + 2 * T, :]
+
     def edge_copies():
         top, bottom = groups - 1, 0
         parts = (
             (0, top, 1, sp.at[0, :, rows - T : rows, :], forcing.at[0:own, TOP - T : TOP, :]),
-            (0, top, 1, trim_s.at[0], trim_r.at[0]),
+            (0, top, 1, trim_s.at[2], trim_r.at[0, 0]),
             (1, bottom, groups - 2, sp.at[1, :, 0:T, :], forcing.at[0:own, oend : oend + T, :]),
-            (1, bottom, groups - 2, trim_s.at[1], trim_r.at[0]),
+            (1, bottom, groups - 2, trim_s.at[1], trim_r.at[0, 0]),
         )
         return [
             (
@@ -768,77 +810,85 @@
             for way, source, target, src, dst in parts
         ]
 
-    back_rows = own * rows + 2 * T
     edge_rows = own * T + 2 * T
 
     receive_rows(0, 8 * T)
     icols_a = pack(0)
     receive_rows(2, 3 * T)
     ocols = pack_ocean()
-    flow_wait(0, 0)
-    fcols_a = pack_flow(0)
+    flow_wait(0, 0, 0)
+    fcols_a = pack_flow(0, 0)
     receive_all(icols_a, ti, tiles)
     prep(0)
     receive_all(ocols, ti, tiles)
     prepare_ocean()
     receive_rows(1, 8 * T)
     icols_b = pack(1)
-    flow_wait(0, 1)
+    flow_wait(0, 0, 1)
     receive_all(fcols_a, ti, tiles)
-    add_flow(0)
-    subcycles(0, 0, NSUB // 2)
-    flow_wait(1, 0)
-    fcols_b = pack_flow(1)
-    subcycles(0, NSUB // 2, NSUB)
-    drag(0)
-    output(0)
+    add_flow(0, 0)
+    subcycles(0, 0, 0, NSUB // 2)
+    flow_wait(1, 0, 0)
+    fcols_b = pack_flow(1, 0)
+    subcycles(0, 0, NSUB // 2, NSUB)
+    drag(0, 0)
+    output(0, 0)
     receive_all(icols_b, ti, tiles)
     prep(1)
-    flow_wait(1, 1)
+    flow_wait(1, 0, 1)
     receive_all(fcols_b, ti, tiles)
-    add_flow(1)
-    subcycles(1, 0, NSUB)
-    drag(1)
-    output(1)
-
-    def rim_of(source, k):
+    add_flow(1, 0)
+    flow_wait(1, 1, 0)
+    fcols_c = pack_flow(1, 1)
+    subcycles(1, 0, 0, NSUB)
+    drag(1, 0)
+    flow_wait(1, 1, 1)
+    receive_all(fcols_c, ti, tiles)
+    add_flow(1, 1)
+    subcycles(1, 1, 0, NSUB)
+    drag(1, 1)
+    output(1, 0)
+    output(1, 1)
+
+    def rim_of(source, part, k):
         lanes_each = L // (2 * (rows // T))
         turn = (lanes_each + 2 * lanes_each * k) % L
-        value = pltpu.roll(trim_r[source, 0], (L - turn) % L, 1)
+        value = pltpu.roll(trim_r[source, part, 0], (L - turn) % L, 1)
         return jnp.where((lane < lanes_each) | (lane >= L - lanes_each), value, 0.0)
 
-    def carry_over(row, source):
+    def carry_over(row, source, part):
         for j in range(span):
             at = (j, slice(row, row + 1), slice(None))
-            forcing[at] = forcing[at] - trim_r[source, 1, j : j + 1, :]
+            forcing[at] = forcing[at] - trim_r[source, part, 1, j : j + 1, :]
 
     for cap, home in enumerate(homes):
 
         @pl.when(gi == home)
         def _():
-            early = [k for k in range(groups) if k != home and (k + cap) % 2 == 0]
-            late = [k for k in range(groups) if k != home and (k + cap) % 2 == 1]
-            for some in ([home] + early, late):
+            early = [k for k in range(groups) if (k + cap) % 2 == 0]
+            late = [k for k in range(groups) if (k + cap) % 2 == 1]
+            for phase, part, some in ((0, 0, early), (1, 0, late), (1, 1, late)):
+                first, last = owned_rows(phase, part)
                 for source in some:
                     if source != home:
-                        take(w0.at[0, 0:back_rows, :], back_recv.at[source])
+                        take(back_bytes(phase, part), back_recv.at[source, part])
                 for source in some:
-                    for k in range(rows // T):
+                    for k in range(first // T, last // T):
                         row = TOP + source * rows + k * T
-                        forcing[own, row : row + T, :] = rim_of(source, k)
+                        forcing[own, row : row + T, :] = rim_of(source, part, k)
             for source in range(groups):
-                carry_over(TOP + (source + 1) * rows, source)
+                carry_over(TOP + (source + 1) * rows, source, int(source in late))
 
     @pl.when(gi == 1)
     def _():
         take(w0.at[0, 0:edge_rows, :], edge_recv)
-        forcing[own, TOP - T : TOP, :] = rim_of(0, rows // T - 1)
-        carry_over(TOP, 0)
+        forcing[own, TOP - T : TOP, :] = rim_of(0, 0, rows // T - 1)
+        carry_over(TOP, 0, 0)
 
     @pl.when(gi == groups - 2)
     def _():
         take(w0.at[0, 0:edge_rows, :], edge_recv)
-        forcing[own, oend : oend + T, :] = rim_of(0, 0)
+        forcing[own, oend : oend + T, :] = rim_of(0, 0, 0)
 
     zero = jnp.zeros((T, L), F32)
 
@@ -976,9 +1026,9 @@
             spans = [flow_span(k) for k in range(groups) if k != home]
             take(cur_in.at[:, 0 : sum(hi - lo for lo, hi, _ in spans), :], flow_send)
 
-    for phase in range(2):
+    for phase, part in ((0, 0), (1, 0), (1, 1)):
         pl.when(gi != lax.rem(gi + phase, 2) * (groups - 1))(
-            lambda: take(w0.at[0, 0:back_rows, :], back_send.at[phase])
+            lambda: take(back_bytes(phase, part), back_send.at[phase + part])
         )
     pl.when((gi == 0) | (gi == groups - 1))(lambda: take(w0.at[0, 0:edge_rows, :], edge_send))
     take(red_r.at[1:count], red_send)
@@ -1007,7 +1057,7 @@
     hbm = pl.BlockSpec(memory_space=pltpu.HBM)
     vmem = pl.BlockSpec(memory_space=pltpu.VMEM)
     dma = pltpu.SemaphoreType.DMA
-    ice = pltpu.VMEM((2, span, irows + PAD, L), F32)
+    ice = pltpu.VMEM((4, span, irows + 16, L), F32)
     ocean = pltpu.VMEM((span, erows + PAD, L), F32)
     plain = pltpu.VMEM((erows, cols), F32)
     results = pl.pallas_call(
@@ -1031,9 +1081,10 @@
             plain,
             plain,
         ]
-        + [ice] * 8
+        + [pltpu.VMEM((4, span, irows + 16, L), F32)] * 5
+        + [ice] * 3
         + [
-            pltpu.VMEM((2, 2, span, irows + PAD, L), F32),
+            pltpu.VMEM((2, 4, span, irows + 16, L), F32),
             pltpu.VMEM((2, 2, irows, L), F32),
         ]
         + [ocean] * 13
@@ -1047,19 +1098,19 @@
             pltpu.VMEM((2, orows + 2 * T, L), F32),
             pltpu.VMEM((2, orows + 2 * T, L), F32),
             pltpu.VMEM((2, span - 1, rows, L), F32),
-            pltpu.VMEM((2, 2, T, L), F32),
-            pltpu.VMEM((groups, 2, T, L), F32),
+            pltpu.VMEM((3, 2, T, L), F32),
+            pltpu.VMEM((groups, 2, 2, T, L), F32),
             pltpu.VMEM((1, L), F32),
             pltpu.VMEM((groups * tiles, 1, L), F32),
             dma((9,)),
             dma,
-            dma((4,)),
+            dma((8,)),
             dma((2,)),
             dma((6,)),
             dma((2,)),
-            dma((10,)),
-            dma((2,)),
-            dma((groups,)),
+            dma((12,)),
+            dma((3,)),
+            dma((groups, 2)),
             dma,
             dma,
             dma,

time: 44.6 us -> 43.9 us (0.984)
  Pallas kernels: 43.8 us -> 43.1 us
    pallas_call x1, Pallas kernels: 42.6 us -> 41.9 us  [step(): pl.pallas_call(functools.partial(kernel, groups, tiles), out_shape=(pltpu...]
where the time goes in v5:
time: 43.9 us; the launch traced here: 43.8 us
  Pallas kernels  43.1 us (98%)
  between operations  0.64 us (1%)
    pallas_call x1, Pallas kernels, step(): pl.pallas_call(functools.partial(kernel, groups, tiles), out_shape=(pltpu...  41.9 us
    pallas_call x1, Pallas kernels, step(): pl.pallas_call(deliver, out_shape=tuple((jax.ShapeDtypeStruct(r.shape, F3...  1.25 us

profile of v5, /device:TPU:0, one launch (start us, length us, event | category | flops | bytes accessed | tf_op | source)
XLA Modules:
  0.0 43.8 jit_solution(10245692806721744207)
XLA Ops:
  0.6 41.9 %shard_map.121 = (f32[256,512]{1,0:T(8,128)S(1)}, f32[2,2,64,512]{3,2,1,0:T(8,128)S(1)}, f32[3,2,64,512]{3,2,1,0:T(8,128)S(1)}) custom-call(f32[256,512]{1,0:T(8,128)} %base_in.1, f32[256,512]{1,0:T(8,128)} %depth_in.1, f32[256,512]{1,0:T(8,128)} %ssh_in.1, f32[2,256,512]{2,1,0:T(8,128)} %cur_in.1, s32[32,64]{1,0:T(8,128)} %land_in.1, ...), custom_call_target="tpu_custom_call" | custom-call | tf_op jit(solution)/shard_map/pallas_call | solution.py:1063
  42.5 1.3 %shard_map.122 = (f32[256,512]{1,0:T(8,128)}, f32[2,2,64,512]{3,2,1,0:T(8,128)}, f32[3,2,64,512]{3,2,1,0:T(8,128)}) custom-call(f32[256,512]{1,0:T(8,128)S(1)} %get-tuple-element.6.refs_0_, f32[2,2,64,512]{3,2,1,0:T(8,128)S(1)} %get-tuple-element.7.refs_1_, f32[3,2,64,512]{3,2,1,0:T(8,128)S(1)} %get-tuple-element.8.refs_2_), custom_call_target="tpu_custom_call" | custom-call | tf_op jit(solution)/shard_map/pallas_call | solution.py:1124

commit v6 on v5

--- a/solution.py
+++ b/solution.py
@@ -152,7 +152,7 @@
     span = own + 1
     ichunks = rows // T + 2
     ochunks = orows // T + 2
-    split = rows - 2 * T
+    split = rows - 3 * T
     above_split, below_split = (0, split // T + 2), (split // T, ichunks)
 
     barrier = pltpu.get_barrier_semaphore()
@@ -673,7 +673,7 @@
                     momentum(k - behind)
             return 0
 
-        lax.fori_loop(first, last, subcycle, 0, unroll=2)
+        lax.fori_loop(first, last, subcycle, 0, unroll=4)
 
     def owned_rows(phase, part):
         if phase == 0:

time: 43.9 us -> 43.3 us (0.986)
  Pallas kernels: 43.1 us -> 42.6 us
    pallas_call x1, Pallas kernels: 41.9 us -> 41.3 us  [step(): pl.pallas_call(functools.partial(kernel, groups, tiles), out_shape=(pltpu...]
where the time goes in v6:
time: 43.3 us; the launch traced here: 43.2 us
  Pallas kernels  42.6 us (98%)
  between operations  0.64 us (1%)
    pallas_call x1, Pallas kernels, step(): pl.pallas_call(functools.partial(kernel, groups, tiles), out_shape=(pltpu...  41.3 us
    pallas_call x1, Pallas kernels, step(): pl.pallas_call(deliver, out_shape=tuple((jax.ShapeDtypeStruct(r.shape, F3...  1.25 us

profile of v6, /device:TPU:0, one launch (start us, length us, event | category | flops | bytes accessed | tf_op | source)
XLA Modules:
  0.0 43.2 jit_solution(16562497991838399305)
XLA Ops:
  0.6 41.3 %shard_map.121 = (f32[256,512]{1,0:T(8,128)S(1)}, f32[2,2,64,512]{3,2,1,0:T(8,128)S(1)}, f32[3,2,64,512]{3,2,1,0:T(8,128)S(1)}) custom-call(f32[256,512]{1,0:T(8,128)} %base_in.1, f32[256,512]{1,0:T(8,128)} %depth_in.1, f32[256,512]{1,0:T(8,128)} %ssh_in.1, f32[2,256,512]{2,1,0:T(8,128)} %cur_in.1, s32[32,64]{1,0:T(8,128)} %land_in.1, ...), custom_call_target="tpu_custom_call" | custom-call | tf_op jit(solution)/shard_map/pallas_call | solution.py:1063
  41.9 1.3 %shard_map.122 = (f32[256,512]{1,0:T(8,128)}, f32[2,2,64,512]{3,2,1,0:T(8,128)}, f32[3,2,64,512]{3,2,1,0:T(8,128)}) custom-call(f32[256,512]{1,0:T(8,128)S(1)} %get-tuple-element.6.refs_0_, f32[2,2,64,512]{3,2,1,0:T(8,128)S(1)} %get-tuple-element.7.refs_1_, f32[3,2,64,512]{3,2,1,0:T(8,128)S(1)} %get-tuple-element.8.refs_2_), custom_call_target="tpu_custom_call" | custom-call | tf_op jit(solution)/shard_map/pallas_call | solution.py:1124
